TPU v7x, 256 devices: a whole 4x4x8 slice. The times are simulated.
256 devices in a mesh: ctx: 32 (over x, y, core), tp: 8 (over z).
Axes of the slice: x: 4, y: 4, z: 8, core: 2. Of those that a mesh axis runs over, the one named last changes fastest.
Arguments:
- patches: bfloat16 [16384, 1280], P('ctx'), may hold values from -21 to 21
- window_ids: int32 [16384], P('ctx'), may hold values from -1 to 4095, as said below
- positions: int32 [4096], P('ctx'), may hold values from 0 to 32768, as said below
- text_embed: bfloat16 [32768, 8192], P('ctx', 'tp'), may hold values from -6 to 6
- cotangent: bfloat16 [32768, 8192], P('ctx', 'tp'), may hold values from -0.119628906 to 0.119628906
- qkv_weight: bfloat16 [3, 1280, 1280], P(None, None, 'tp'), may hold values from -0.15625 to 0.15625
- out_weight: bfloat16 [1280, 1280], P('tp'), may hold values from -0.15625 to 0.15625
- merger_weight: bfloat16 [5120, 8192], P('ctx', 'tp'), may hold values from -0.078125 to 0.078125
- norm_gain: bfloat16 [8192], P('tp'), may hold values from 0.099609375 to 1.8984375
Outputs:
- normed: bfloat16 [32768, 8192], P('ctx', 'tp')
- merger_grad: float32 [5120, 8192], P('ctx', 'tp')
Inputs may be any that keep to these rules, and one draw needn't show every extreme that they name: `window_ids`: windows are runs of consecutive patch slots of one index of ctx, each of 4 to 64 slots and a multiple of 4; every window id belongs to one index of ctx; the padding slots of an index of ctx come after its live slots and carry -1. Merged slot j of an index of ctx covers its patch slots 4j to 4j+3 and is live exactly when those are; live slots carry distinct positions, dead ones carry 32768. The live slots of one index of ctx name at most 4 positions among the 1024 positions of any one index of ctx.
All inputs are finite; a program needn't handle non-finite values.
Results may differ from a plain program's by a relative error of at most 0.014.
Values may be sent and summed in bfloat16 or wider, within the bound.
A program may use at most 128 MiB of HBM per device.

v0:
```python
import jax
import jax.numpy as jnp
from jax import lax
from jax.sharding import PartitionSpec as P

D = 8192
HEAD_DIM = 80


def sent_to_all(shard, axis):
    copies = jnp.broadcast_to(shard, (lax.axis_size(axis), *shard.shape))
    return lax.all_to_all(copies, axis, split_axis=0, concat_axis=0, tiled=True)


def taken_together(shard, axis):
    return sent_to_all(shard, axis).sum(axis=0)


def in_one(arrays, axis):
    ends = [0]
    for a in arrays:
        ends.append(ends[-1] + a.size)
    so_far = taken_together(jnp.concatenate([a.ravel() for a in arrays]), axis)
    return tuple((so_far[b:e].reshape(a.shape) for a, b, e in zip(arrays, ends, ends[1:])))


def window_attention(patches, window_ids, qkv_weight):
    slot_rows = patches.shape[0]
    projected = [
        jnp.dot(patches, qkv_weight[i], preferred_element_type=jnp.float32).astype(jnp.bfloat16)
        for i in range(3)
    ]
    local_heads = qkv_weight.shape[2] // HEAD_DIM
    queries = projected[0].reshape(slot_rows, local_heads, HEAD_DIM)
    keys_all = projected[1].reshape(slot_rows, local_heads, HEAD_DIM)
    values = projected[2].reshape(slot_rows, local_heads, HEAD_DIM)
    width = min(512, slot_rows)
    factor = 1.0 / HEAD_DIM**0.5

    def one_block(block_index):
        scores = (
            jnp.einsum("qhd,khd->hqk", queries, keys_all, preferred_element_type=jnp.float32)
            * factor
        )
        allowed = (window_ids[:, None] == window_ids[None, :]) & (window_ids[None, :] >= 0)
        scores = jnp.where(allowed[None], scores, jnp.float32(-1e30))
        highest = jnp.max(scores, axis=2, keepdims=True)
        weights = jnp.exp(scores - highest)
        probs = (weights / jnp.sum(weights, axis=2, keepdims=True)).astype(jnp.bfloat16)
        attended = jnp.einsum("hqk,khd->qhd", probs, values, preferred_element_type=jnp.float32)
        return attended.astype(jnp.bfloat16).reshape(width, local_heads * HEAD_DIM)

    blocks = lax.map(one_block, jnp.arange(slot_rows // width, dtype=jnp.int32))
    return blocks.reshape(slot_rows, local_heads * HEAD_DIM)


def contract_rows(left, right):
    return lax.dot_general(
        left, right, (((0,), (0,)), ((), ())), preferred_element_type=jnp.float32
    )


def shards(
    patches,
    window_ids,
    positions,
    text_embed,
    cotangent,
    qkv_weight,
    out_weight,
    merger_weight,
    norm_gain,
):
    ctx_size = lax.axis_size("ctx")
    slots = positions.shape[0]
    tok_rows = text_embed.shape[0]
    bucket_size = slots // ctx_size
    attended = window_attention(patches, window_ids, qkv_weight)
    partial_out = jnp.dot(attended, out_weight, preferred_element_type=jnp.float32)
    summed = lax.psum(partial_out.astype(jnp.bfloat16), "tp").astype(jnp.float32)
    hidden = (patches.astype(jnp.float32) + summed).astype(jnp.bfloat16)
    merged_in = hidden.reshape(slots, 4 * hidden.shape[1])
    columns = lax.all_to_all(merged_in, "ctx", split_axis=1, concat_axis=0, tiled=True)
    chosen = merged_in
    merged = jnp.dot(
        chosen,
        lax.all_gather(merger_weight, "ctx", axis=0, tiled=True),
        preferred_element_type=jnp.float32,
    ).astype(jnp.bfloat16)
    target = positions // tok_rows
    hits = (target[:, None] == jnp.arange(ctx_size, dtype=jnp.int32)[None, :]).astype(jnp.int32)
    ranks = jnp.sum(jnp.cumsum(hits, axis=0) * hits, axis=1) - 1
    bucket = jnp.where(target < ctx_size, target * bucket_size + ranks, -1)
    select = jnp.arange(slots, dtype=jnp.int32)[:, None] == bucket[None, :]
    select_mat = select.astype(jnp.bfloat16)
    outgoing = jnp.dot(select_mat, merged, preferred_element_type=jnp.float32).astype(jnp.bfloat16)
    local_row = positions % tok_rows
    occupied = jnp.any(select, axis=1)
    out_rows = jnp.where(occupied, jnp.sum(jnp.where(select, local_row[None, :], 0), axis=1), -1)
    incoming, in_rows = (
        lax.all_to_all(outgoing, "ctx", split_axis=0, concat_axis=0, tiled=True),
        lax.all_to_all(out_rows, "ctx", split_axis=0, concat_axis=0, tiled=True),
    )
    placed = jnp.arange(tok_rows, dtype=jnp.int32)[:, None] == in_rows[None, :]
    placed_mat = placed.astype(jnp.bfloat16)
    vision = jnp.dot(placed_mat, incoming, preferred_element_type=jnp.float32)
    is_vision = jnp.any(placed, axis=1)
    embedded = jnp.where(is_vision[:, None], vision, text_embed.astype(jnp.float32))
    gain_vec = norm_gain.astype(jnp.float32)[None, :]
    gained = gain_vec * cotangent.astype(jnp.float32)
    squares, inner = in_one(
        (jnp.sum(embedded * embedded, axis=1), jnp.sum(embedded * gained, axis=1)), "tp"
    )
    scale = lax.rsqrt(squares / D + 1e-06)[:, None]
    normed = (embedded * scale * gain_vec).astype(jnp.bfloat16)
    d_embed = (scale * gained - embedded * scale**3 * inner[:, None] / D).astype(jnp.bfloat16)
    back_rows = contract_rows(placed_mat, d_embed).astype(jnp.bfloat16)
    returned = lax.all_to_all(back_rows, "ctx", split_axis=0, concat_axis=0, tiled=True)
    d_merged = contract_rows(select_mat, returned).astype(jnp.bfloat16)
    chosen = columns
    merger_grad = contract_rows(chosen, lax.all_gather(d_merged, "ctx", axis=0, tiled=True))
    return (normed, merger_grad)


def solution(mesh):
    in_specs = (
        P("ctx", None),
        P("ctx"),
        P("ctx"),
        P("ctx", "tp"),
        P("ctx", "tp"),
        P(None, None, "tp"),
        P("tp", None),
        P("ctx", "tp"),
        P("tp"),
    )
    out_specs = (P("ctx", "tp"), P("ctx", "tp"))
    return jax.shard_map(shards, mesh=mesh, in_specs=in_specs, out_specs=out_specs, check_vma=False)
```

profile of v0, /device:TPU:1, one launch (start us, length us, event | category | flops | bytes accessed | tf_op | source)
XLA Modules:
  0.0 239.2 jit_solution(6177392035362610401)
XLA Ops:
  8.1 2.1 convolution_convert_fusion.7
  10.2 2.0 convolution_convert_fusion.5
  12.2 1.6 convolution_convert_fusion.6
  15.0 1.2 convolution_convert_fusion.4
  16.3 1.6 convolution_convert_fusion
  19.9 8.6 %all-to-all-start = ((s32[32,4,1]{1,2,0:T(1,128)}), s32[32,4,1]{1,2,0:T(1,128)S(1)}, u32[]{:S(2)}, u32[]{:S(2)}) async-start(s32[32,4,1]{1,2,0:T(1,128)} %bitcast), calls=%async_computation | async-start | bytes 32768 | tf_op jit(solution)/shard_map/all_to_all | solution.py:102
  28.5 66.8 %all-reduce.2.cloned.1.call-done = bf16[512,1280]{1,0:T(8,128)(2,1)} async-done(((bf16[512,1280]{1,0:T(8,128)(2,1)}), bf16[512,1280]{1,0:T(8,128)(2,1)}) %all-reduce.2.cloned.1.call-update) | async-done | bytes 1310736 | tf_op jit(solution)/shard_map/psum | solution.py:80
  95.3 1.6 add_convert_fusion
  97.8 5.7 %convolution_convert_fusion.2 = bf16[128,1024]{1,0:T(8,128)(2,1)S(1)} fusion(bf16[128,5120]{1,0:T(8,128)(2,1)S(1)} %reshape.118, bf16[5120,1024]{1,0:T(8,128)(2,1)} %all-gather.3.cloned.1.call-done, s32[128]{0:T(128)S(1)} %compare_select_fusion), kind=kOutput, calls=%fused_computation.19 | convolution fusion | flops 1376010240 | bytes 12059136 | tf_op jit(solution)/shard_map/dot_general | solution.py:96
  104.3 11.4 %all-to-all-start.1 = ((bf16[32,4,1024]{2,1,0:T(4,128)(2,1)}), bf16[32,4,1024]{2,1,0:T(4,128)(2,1)S(1)}, u32[]{:S(2)}, u32[]{:S(2)}) async-start(bf16[32,4,1024]{2,1,0:T(4,128)(2,1)} %all_to_all.39), calls=%async_computation.1 | async-start | bytes 524288 | tf_op jit(solution)/shard_map/all_to_all | solution.py:101
  115.8 3.9 %copy.37 = bf16[1024,1024]{0,1:T(8,128)(2,1)} copy(bf16[1024,1024]{1,0:T(8,128)(2,1)} %param.13) | data formatting | bytes 4194304 | tf_op args[4]
  119.7 4.0 %copy.36 = bf16[1024,1024]{0,1:T(8,128)(2,1)} copy(bf16[1024,1024]{1,0:T(8,128)(2,1)} %param.12) | data formatting | bytes 4194304 | tf_op args[3]
  125.2 5.6 %multiply_reduce_fusion.1 = (f32[1024]{0:T(1024)S(1)}, f32[1024]{0:T(1024)S(1)}, f32[1024,1024]{0,1:T(8,128)}) fusion(bf16[1024,1024]{0,1:T(8,128)(2,1)} %copy.37, f32[1024]{0:T(1024)S(1)} %convert_element_type.78, bf16[1024,1024]{0,1:T(8,128)(2,1)} %copy.36, bf16[128,1024]{1,0:T(8,128)(2,1)S(1)} %all_to_all.41, s32[128]{0:T(128)S(1)} %eq.74, ...), kind=kOutput, calls=%fused_computation.5 | convolution fusion | flops 276953088 | bytes 8664576 | tf_op jit(solution)/shard_map/dot_general | solution.py:106
  130.9 11.2 %all_to_all.55 = f32[8,1,2048]{2,1,0:T(1,128)S(1)} all-to-all(f32[8,1,2048]{2,1,0:T(1,128)S(1)} %broadcast_in_dim.73), channel_id=1, replica_groups=mesh['ctx'=32,'tp'=8] {'tp'}, dimensions={0} | all-to-all | bytes 131072 | tf_op jit(solution)/shard_map/all_to_all | solution.py:12
  142.2 4.3 %fusion.6 = bf16[128,1024]{1,0:T(8,128)(2,1)S(1)} fusion(f32[1024,1024]{0,1:T(8,128)} %get-tuple-element.37, bf16[1024,1024]{0,1:T(8,128)(2,1)} %copy.37, f32[1024]{0:T(1024)S(1)} %get-tuple-element.34, f32[1024]{0:T(1024)S(1)} %get-tuple-element.32, f32[1024]{0:T(1024)S(1)} %get-tuple-element.33, f32[1024]{0:T(1024)S(1)} %convert_element_type.78, ...), kind=kOutput, calls=%fused_computation.17 | convolution fusion | flops 277217280 | bytes 6570496 | tf_op jit(solution)/shard_map/dot_general | solution.py:58
  146.5 17.6 %all_to_all.56 = bf16[32,4,1024]{2,1,0:T(4,128)(2,1)S(1)} all-to-all(bf16[32,4,1024]{2,1,0:T(4,128)(2,1)S(1)} %all_to_all.47), channel_id=1, replica_groups=mesh['ctx'=32,'tp'=8] {'ctx'}, dimensions={0} | all-to-all | bytes 524288 | tf_op jit(solution)/shard_map/all_to_all | solution.py:118
  165.2 3.6 %all_to_all.43 = bf16[128,32,160]{2,1,0:T(8,128)(2,1)} reshape(bf16[512,1280]{1,0:T(8,128)(2,1)S(1)} %add_convert_fusion) | data formatting | bytes 2621440 | tf_op jit(solution)/shard_map/all_to_all | solution.py:83
  168.8 4.4 %copy.39 = bf16[128,32,160]{0,2,1:T(8,128)(2,1)} copy(bf16[128,32,160]{2,1,0:T(8,128)(2,1)} %all_to_all.43) | data formatting | bytes 2621440 | tf_op jit(solution)/shard_map/all_to_all | solution.py:83
  173.2 4.5 %all-to-all-start.3 = ((bf16[128,32,160]{0,2,1:T(8,128)(2,1)}), bf16[128,32,160]{0,2,1:T(8,128)(2,1)}, u32[]{:S(2)}, u32[]{:S(2)}) async-start(bf16[128,32,160]{0,2,1:T(8,128)(2,1)} %copy.39), calls=%async_computation.3 | async-start | bytes 2621440 | tf_op jit(solution)/shard_map/all_to_all | solution.py:83
  177.7 2.6 %multiply_convert_fusion = bf16[1024,1024]{0,1:T(8,128)(2,1)S(1)} fusion(f32[1024,1024]{0,1:T(8,128)} %get-tuple-element.37, f32[1024]{0:T(1024)S(1)} %get-tuple-element.33, f32[1024]{0:T(1024)S(1)} %convert_element_type.78), kind=kLoop, calls=%fused_computation.2 | loop fusion | flops 3145728 | bytes 6299648 | tf_op jit(solution)/shard_map/convert_element_type | solution.py:115
  180.3 2.6 %copy.41 = bf16[1024,1024]{1,0:T(8,128)(2,1)} copy(bf16[1024,1024]{0,1:T(8,128)(2,1)S(1)} %multiply_convert_fusion) | data formatting | bytes 4194304
  182.9 15.3 %all-to-all-done.3 = bf16[128,32,160]{0,2,1:T(8,128)(2,1)} async-done(((bf16[128,32,160]{0,2,1:T(8,128)(2,1)}), bf16[128,32,160]{0,2,1:T(8,128)(2,1)}, u32[]{:S(2)}, u32[]{:S(2)}) %all-to-all-start.3) | async-done | bytes 1310752 | tf_op jit(solution)/shard_map/all_to_all | solution.py:83
  198.2 27.4 %all-gather.5.cloned.1.call-done = bf16[4096,1024]{1,0:T(8,128)(2,1)} async-done(((bf16[128,1024]{1,0:T(8,128)(2,1)}), bf16[4096,1024]{1,0:T(8,128)(2,1)}) %all-gather.5.cloned.1.call-update) | async-done | bytes 8388624 | tf_op jit(solution)/shard_map/all_gather | solution.py:121
  225.6 6.2 %fusion.3 = f32[160,1024]{1,0:T(8,128)} fusion(bf16[4096,1024]{1,0:T(8,128)(2,1)} %all-gather.5.cloned.1.call-done, bf16[128,32,160]{0,2,1:T(8,128)(2,1)} %all-to-all-done.3), kind=kOutput, calls=%fused_computation.14 | convolution fusion | flops 1342177280 | bytes 10354688 | tf_op jit(solution)/shard_map/dot_general | solution.py:58
  (46 shorter events, 7.8 us)
Async XLA Ops:
  8.0 8.3 %copy-start = (bf16[160,1280]{1,0:T(8,128)(2,1)S(1)}, bf16[160,1280]{1,0:T(8,128)(2,1)}, u32[]{:S(2)}) copy-start(bf16[160,1280]{1,0:T(8,128)(2,1)} %param.15) | copy-start | bytes 1228804
  8.0 4.1 %copy-start.1 = (bf16[512,1280]{1,0:T(8,128)(2,1)S(1)}, bf16[512,1280]{1,0:T(8,128)(2,1)}, u32[]{:S(2)}) copy-start(bf16[512,1280]{1,0:T(8,128)(2,1)} %param.9) | copy-start | bytes 3932164
  8.0 87.3 %all-reduce.2.cloned.1.call-start = ((), (), s32[]{:S(2)}) async-start(), calls=%async_computation.5 | async-start | bytes 2621440 | tf_op jit(solution)/shard_map/psum | solution.py:80
  10.2 3.6 %copy-start.2 = (s32[512]{0:T(512)S(1)}, s32[512]{0:T(512)}, u32[]{:S(2)}) copy-start(s32[512]{0:T(512)} %param.10) | copy-start | bytes 6148
  16.2 2.2 copy-start.4
  17.9 79.9 %all-gather.3.cloned.1.call-start = ((), (), s32[]{:S(2)}) async-start(), calls=%async_computation.6 | async-start | bytes 10813440 | tf_op jit(solution)/shard_map/all_gather | solution.py:87
  19.9 84.4 %all-to-all-start = ((s32[32,4,1]{1,2,0:T(1,128)}), s32[32,4,1]{1,2,0:T(1,128)S(1)}, u32[]{:S(2)}, u32[]{:S(2)}) async-start(s32[32,4,1]{1,2,0:T(1,128)} %bitcast), calls=%async_computation | async-start | bytes 32768 | tf_op jit(solution)/shard_map/all_to_all | solution.py:102
  97.8 18.0 %copy-start.3 = (bf16[1024]{0:T(1024)(128)(2,1)S(1)}, bf16[1024]{0:T(1024)(128)(2,1)}, u32[]{:S(2)}) copy-start(bf16[1024]{0:T(1024)(128)(2,1)} %param.17) | copy-start | bytes 6148
  104.3 20.9 %all-to-all-start.1 = ((bf16[32,4,1024]{2,1,0:T(4,128)(2,1)}), bf16[32,4,1024]{2,1,0:T(4,128)(2,1)S(1)}, u32[]{:S(2)}, u32[]{:S(2)}) async-start(bf16[32,4,1024]{2,1,0:T(4,128)(2,1)} %all_to_all.39), calls=%async_computation.1 | async-start | bytes 524288 | tf_op jit(solution)/shard_map/all_to_all | solution.py:101
  115.7 109.9 %all-gather.5.cloned.1.call-start = ((), (), s32[]{:S(2)}) async-start(), calls=%async_computation.7 | async-start | bytes 8650752 | tf_op jit(solution)/shard_map/all_gather | solution.py:121
  173.2 25.0 %all-to-all-start.3 = ((bf16[128,32,160]{0,2,1:T(8,128)(2,1)}), bf16[128,32,160]{0,2,1:T(8,128)(2,1)}, u32[]{:S(2)}, u32[]{:S(2)}) async-start(bf16[128,32,160]{0,2,1:T(8,128)(2,1)} %copy.39), calls=%async_computation.3 | async-start | bytes 2621440 | tf_op jit(solution)/shard_map/all_to_all | solution.py:83
Sparse Core Ops, SparseCore 0:
  18.0 77.2 all-reduce.1
Sparse Core Ops, SparseCore 1:
  20.9 66.7 all-gather.2
  165.3 60.3 all-gather.4
where the time goes:
time: 240 us; the launch traced here: 239 us
  waiting for transfers between devices  110 us (46%)
  matrix products  32.1 us (13%)
  blocking collectives  28.8 us (12%)
  starting transfers between devices  24.6 us (10%)
  local copies, waits for them, and re-layouts  21.8 us (9%)
  between operations  15.8 us (7%)
  other arithmetic  6.13 us (3%)
    psum x1, waiting for transfers between devices, shards(): lax.psum(partial_out.astype(jnp.bfloat16), 'tp').astype(jnp.float32)  66.8 us
    all_gather x1, waiting for transfers between devices, shards(): lax.all_gather(d_merged, 'ctx', axis=0, tiled=True)  27.4 us
    all_to_all x1, blocking collectives, shards(): lax.all_to_all(back_rows, 'ctx', split_axis=0, concat_axis=0, tiled=True)  17.6 us
    all_to_all x1, waiting for transfers between devices, shards(): lax.all_to_all(merged_in, 'ctx', split_axis=1, concat_axis=0, tiled=True)  15.3 us
    all_to_all x1, starting transfers between devices, shards(): lax.all_to_all(outgoing, 'ctx', split_axis=0, concat_axis=0, tiled=True)  11.4 us
    dot_general x3, matrix products, contract_rows(): lax.dot_general(left, right, (((0,), (0,)), ((), ())), preferred_element_...  11.4 us
    all_to_all x1, blocking collectives, sent_to_all(): return lax.all_to_all(copies, axis, split_axis=0, concat_axis=0, tiled=True)  11.2 us
    unnamed x13, local copies, waits for them, and re-layouts  10.5 us
  transfers between devices with their start and end apart: 6, of which 3 were waited for; matrix products, arithmetic and copies ran while one was open for 12% of the time, Pallas kernels for 0%

commit v1 on v0

v1 whole, which is shorter than its diff:
```python
import jax
import jax.numpy as jnp
from jax import lax
from jax.experimental import pallas as pl
from jax.experimental.pallas import tpu as pltpu
from jax.sharding import PartitionSpec as P

MESH = pl.DeviceIdType.MESH
D = 8192
HEAD_DIM = 80
NX, NY, NC, NZ = 4, 4, 2, 8
N_CTX = 32
SLOTS = 128
TOK = 1024
DV = 1280
HCOLS = 160
ROWS_W = 160
F32 = jnp.float32
BF16 = jnp.bfloat16


def remote(src, dst, send, recv, dev):
    return pltpu.make_async_remote_copy(
        src_ref=src, dst_ref=dst, send_sem=send, recv_sem=recv, device_id=dev, device_id_type=MESH
    )


def dot(a, b):
    return jnp.dot(a, b, preferred_element_type=F32)


def dot_nt(a, b):
    return lax.dot_general(a, b, (((1,), (1,)), ((), ())), preferred_element_type=F32)


def iota(shape, dim):
    return lax.broadcasted_iota(jnp.int32, shape, dim)


class Place:
    def __init__(self):
        self.ctx = lax.axis_index("ctx")
        self.z = lax.axis_index("tp")
        self.core = self.ctx % 2
        y = (self.ctx // 2) % NY
        x = self.ctx // (2 * NY)
        self.f = x * (1 - self.core) + y * self.core
        self.g = y * (1 - self.core) + x * self.core
        self.sib = self.ctx + 1 - 2 * self.core
        self.offs = (0, 3, 1, 2)

    def ctx_of(self, f, g):
        x = f * (1 - self.core) + g * self.core
        y = g * (1 - self.core) + f * self.core
        return (x * NY + y) * 2 + self.core

    def near(self, df, dg):
        return self.ctx_of((self.f + df) % 4, (self.g + dg) % 4)

    def dev(self, df, dg):
        return {"ctx": self.near(df, dg), "tp": self.z}


class PlaneGather:
    def __init__(self, place, buf, rows, ss, rs):
        self.p, self.buf, self.rows, self.half = place, buf, rows, rows // 2
        self.ss, self.rs = ss, rs
        self.started = []

    def block(self, df, dg, part=None):
        base = self.p.near(df, dg) * self.rows
        if part is None:
            return self.buf.at[pl.ds(pl.multiple_of(base, 32), self.rows), :]
        base = base + part * self.half
        return self.buf.at[pl.ds(pl.multiple_of(base, 16), self.half), :]

    def send(self, n, region, dev):
        c = remote(region, region, self.ss.at[n], self.rs.at[n], dev)
        c.start()
        self.started.append(c)

    def recv(self, n, region):
        remote(region, region, self.ss.at[n], self.rs.at[n], self.p.dev(0, 1)).wait_recv()

    def sibling(self, i, j):
        o = self.p.offs
        self.send(20 + 4 * i + j, self.block(o[i], o[j]), {"ctx": self.p.sib, "tp": self.p.z})

    def item(self, i):
        o = self.p.offs
        self.send(4 + 4 * i, self.block(o[i], 0), self.p.dev(0, 1))
        self.send(5 + 4 * i, self.block(o[i], 0), self.p.dev(0, 3))
        self.sibling(i, 0)

    def start(self):
        own = self.block(0, 0)
        self.send(0, own, self.p.dev(1, 0))
        self.send(1, own, self.p.dev(3, 0))
        self.item(0)

    def first(self):
        self.recv(0, self.block(3, 0))
        self.send(2, self.block(3, 0, 0), self.p.dev(1, 0))
        self.item(1)
        self.recv(1, self.block(1, 0))
        self.send(3, self.block(1, 0, 1), self.p.dev(3, 0))
        self.item(2)

    def second(self):
        self.recv(2, self.block(2, 0, 0))
        self.recv(3, self.block(2, 0, 1))
        self.item(3)

    def third(self, i):
        o = self.p.offs[i]
        self.recv(4 + 4 * i, self.block(o, 3))
        self.send(6 + 4 * i, self.block(o, 3, 0), self.p.dev(0, 1))
        self.sibling(i, 1)
        self.recv(5 + 4 * i, self.block(o, 1))
        self.send(7 + 4 * i, self.block(o, 1, 1), self.p.dev(0, 3))
        self.sibling(i, 2)

    def fourth(self, i):
        o = self.p.offs[i]
        self.recv(6 + 4 * i, self.block(o, 2, 0))
        self.recv(7 + 4 * i, self.block(o, 2, 1))
        self.sibling(i, 3)

    def from_sibling(self, i, j):
        o = self.p.offs
        base = self.p.near(o[i], o[j]) + 1 - 2 * self.p.core
        region = self.buf.at[pl.ds(pl.multiple_of(base * self.rows, 32), self.rows), :]
        self.recv(20 + 4 * j + i, region)

    def pair_rows(self, i, j):
        o = self.p.offs
        return (self.p.near(o[i], o[j]) - self.p.core) * self.rows

    def finish(self):
        for c in self.started:
            c.wait_send()


class Ring:
    def __init__(self, place, region, ss, rs):
        self.p, self.region, self.ss, self.rs = place, region, ss, rs
        self.started = []

    def step(self, s):
        z = self.p.z
        for way in range(2):
            sign = 1 - 2 * way
            part = way if s == 4 else None
            src = self.region((z - sign * (s - 1) + NZ) % NZ, part)
            c = remote(
                src, src, self.ss.at[4 * way + s - 1], self.rs.at[4 * way + s - 1],
                {"ctx": self.p.ctx, "tp": (z + sign + NZ) % NZ},
            )
            c.start()
            self.started.append(c)

    def recv(self, s):
        z = self.p.z
        for way in range(2):
            sign = 1 - 2 * way
            part = way if s == 4 else None
            dst = self.region((z - sign * s + NZ) % NZ, part)
            remote(
                dst, dst, self.ss.at[4 * way + s - 1], self.rs.at[4 * way + s - 1],
                {"ctx": self.p.ctx, "tp": (z + sign + NZ) % NZ},
            ).wait_recv()

    def finish(self):
        for c in self.started:
            c.wait_send()


def kernel(
    pat, wid, pos, text_in, cot_in, qkv, ow_in, w_in, gain,
    normed_out, grad_out,
    wf, gf, owf, attf, att_t, hid, perm, colsend, colin, colf, colg, cols, text, cot, normed,
    q0s, q1s, ks, vts, widc, mrow, rows_send, rows_in, incf, idx_send, idx_in, stats, cotsel, scol, drow,
    local, w_ss, w_rs, g_ss, g_rs, ow_ss, ow_rs, osib_ss, osib_rs, at_ss, at_rs,
    ix_ss, ix_rs, rw_ss, rw_rs, co_ss, co_rs, st_ss, st_rs,
):
    p = Place()
    ctx, z, core = p.ctx, p.z, p.core

    def other(d):
        return (ctx + d) % N_CTX

    def behind(d):
        return (ctx + N_CTX - d) % N_CTX

    barrier = pltpu.get_barrier_semaphore()

    @pl.loop(1, N_CTX)
    def _(d):
        pl.semaphore_signal(barrier, inc=1, device_id={"ctx": other(d), "tp": z}, device_id_type=MESH)

    @pl.loop(1, NZ)
    def _(d):
        pl.semaphore_signal(barrier, inc=1, device_id={"ctx": ctx, "tp": (z + d) % NZ}, device_id_type=MESH)

    own_w = wf.at[pl.ds(pl.multiple_of(ctx * ROWS_W, 32), ROWS_W), :]
    own_ow = owf.at[pl.ds(pl.multiple_of(z * HCOLS, 32), HCOLS), :]
    load_w = pltpu.make_async_copy(w_in, own_w, local.at[0])
    load_ow = pltpu.make_async_copy(ow_in, own_ow, local.at[1])
    load_text = pltpu.make_async_copy(text_in, text, local.at[2])
    load_cot = pltpu.make_async_copy(cot_in, cot, local.at[3])
    load_w.start()
    load_ow.start()
    load_text.start()
    load_cot.start()

    pos_row = pos[...]
    pos_col = jnp.broadcast_to(pos_row, (SLOTS, SLOTS)).T
    t_row = pos_row // TOK
    t_col = pos_col // TOK
    same = t_col == t_row
    earlier_down = same & (iota((SLOTS, SLOTS), 0) < iota((SLOTS, SLOTS), 1))
    earlier_across = same & (iota((SLOTS, SLOTS), 1) < iota((SLOTS, SLOTS), 0))
    rank_row = jnp.sum(jnp.where(earlier_down, 1.0, 0.0).astype(F32), axis=0, keepdims=True)
    rank_col = jnp.sum(jnp.where(earlier_across, 1.0, 0.0).astype(F32), axis=1, keepdims=True)
    live_row = t_row < N_CTX
    bucket_row = jnp.where(live_row, t_row.astype(F32) * 4.0 + rank_row, -1.0)
    to_owner = jnp.where(iota((N_CTX, SLOTS), 0) == t_row, 1.0, 0.0).astype(BF16)
    row_no = pos_col % TOK + 1
    lane_of = rank_col.astype(jnp.int32) * N_CTX + ctx
    at_lane = lane_of == iota((SLOTS, SLOTS), 1)
    high = jnp.where(at_lane, (row_no // 32).astype(F32), 0.0).astype(BF16)
    low = jnp.where(at_lane, (row_no % 32).astype(F32), 0.0).astype(BF16)
    index_rows = (dot(to_owner, high) * 32.0 + dot(to_owner, low)).astype(jnp.int32)
    for t in range(N_CTX):
        idx_send[t] = jnp.broadcast_to(index_rows[t : t + 1, :], (8, SLOTS))
    idx_in[ctx] = idx_send[ctx]

    for b in range(4):
        widc[128 * b : 128 * (b + 1), :] = jnp.broadcast_to(wid[:, 128 * b : 128 * (b + 1)], (128, 128)).T

    pl.semaphore_wait(barrier, N_CTX - 1 + NZ - 1)

    wg = PlaneGather(p, wf, ROWS_W, w_ss, w_rs)
    load_w.wait()
    wg.start()

    def ow_region(zz, part):
        base = pl.multiple_of(zz * HCOLS + core * 80, 16)
        if part is None:
            return owf.at[pl.ds(base, 80), :]
        return owf.at[pl.ds(base, 80), pl.ds(part * 640, 640)]

    def att_region(zz, part):
        if part is None:
            return attf.at[pl.ds(pl.multiple_of(zz * HCOLS, 32), HCOLS), :]
        return attf.at[pl.ds(pl.multiple_of(zz * HCOLS + part * 80, 16), 80), :]

    osib = []

    def ow_to_sibling(k, zz):
        src = ow_region(zz, None)
        c = remote(src, src, osib_ss.at[k], osib_rs.at[k], {"ctx": p.sib, "tp": z})
        c.start()
        osib.append(c)

    og = Ring(p, ow_region, ow_ss, ow_rs)
    ag = Ring(p, att_region, at_ss, at_rs)
    load_ow.wait()
    og.step(1)

    @pl.loop(1, N_CTX)
    def _(d):
        remote(
            idx_send.at[other(d)], idx_in.at[ctx], ix_ss.at[d], ix_rs.at[d], {"ctx": other(d), "tp": z}
        ).start()

    patches = pat[...]
    lane = iota((512, HCOLS), 1)
    q = dot(patches, qkv[0]).astype(BF16).astype(F32)
    q0s[...] = jnp.where(lane < HEAD_DIM, q, 0.0).astype(BF16)
    q1s[...] = jnp.where(lane < HEAD_DIM, 0.0, q).astype(BF16)
    ks[...] = dot(patches, qkv[1]).astype(BF16)
    vts[...] = dot(patches, qkv[2]).astype(BF16).T
    wg.first()

    factor = 1.0 / HEAD_DIM**0.5

    @pl.loop(0, 4)
    def _(b):
        cols_b = pl.ds(pl.multiple_of(b * 128, 128), 128)
        ids = wid[:, cols_b]
        allowed = (widc[...] == ids) & (widc[...] >= 0)
        parts = []
        for qs in (q0s, q1s):
            scores = dot_nt(ks[...], qs[cols_b, :]) * factor
            scores = jnp.where(allowed, scores, -1e30)
            weights = jnp.exp(scores - jnp.max(scores, axis=0, keepdims=True))
            probs = (weights / jnp.sum(weights, axis=0, keepdims=True)).astype(BF16)
            parts.append(dot(vts[...], probs))
        row = iota((HCOLS, 128), 0)
        attf[pl.ds(pl.multiple_of(z * HCOLS, 32), HCOLS), cols_b] = jnp.where(
            row < HEAD_DIM, parts[0], parts[1]
        ).astype(BF16)

    ag.step(1)

    wg.second()
    og.recv(1)
    og.step(2)
    wg.third(0)
    ag.recv(1)
    ag.step(2)
    og.recv(2)
    og.step(3)
    wg.third(1)
    wg.third(2)
    ag.recv(2)
    ag.step(3)
    og.recv(3)
    og.step(4)
    wg.third(3)
    ag.recv(3)
    ag.step(4)
    for k in (0, 1, 2, 4, 5, 6):
        ow_to_sibling(k, (z + 5 + k) % NZ)
    for i in range(4):
        wg.fourth(i)
    og.recv(4)
    ow_to_sibling(7, (z + 4) % NZ)
    ag.recv(4)
    for k in (0, 1, 2, 4, 5, 6, 7):
        zz = (z + 5 + k) % NZ if k < 7 else (z + 4) % NZ
        dst = owf.at[pl.ds(pl.multiple_of(zz * HCOLS + (1 - core) * 80, 16), 80), :]
        remote(dst, dst, osib_ss.at[k], osib_rs.at[k], {"ctx": p.sib, "tp": z}).wait_recv()

    for zz in range(NZ):
        att_t[:, zz * HCOLS : (zz + 1) * HCOLS] = attf[zz * HCOLS : (zz + 1) * HCOLS, :].T

    @pl.loop(0, 5)
    def _(n):
        cols_n = pl.ds(pl.multiple_of(n * 256, 256), 256)
        out = dot(att_t[...], owf[:, cols_n])
        hid[:, cols_n] = (pat[:, cols_n].astype(F32) + out).astype(BF16)

    spread_at = jnp.where(iota((SLOTS, 512), 0) == iota((SLOTS, 512), 1) // 4, 1.0, 0.0).astype(BF16)
    bucket512 = dot(jnp.broadcast_to(bucket_row, (8, SLOTS)).astype(BF16), spread_at)[0:1, :]
    chosen = iota((SLOTS, 512), 0).astype(F32) == bucket512
    for i in range(4):
        select = jnp.where(chosen & (iota((SLOTS, 512), 1) % 4 == i), 1.0, 0.0).astype(BF16)
        for n in range(5):
            perm[:, i * DV + n * 256 : i * DV + (n + 1) * 256] = dot(
                select, hid[:, n * 256 : (n + 1) * 256]
            ).astype(BF16)

    for i in range(4):
        for j in range(4):
            wg.from_sibling(i, j)

    @pl.loop(0, 4)
    def _(n):
        cols_n = pl.ds(pl.multiple_of(n * 256, 256), 256)
        mrow[:, cols_n] = dot(perm[...], wf[:, cols_n]).astype(BF16).astype(F32)

    @pl.loop(0, N_CTX // 2)
    def _(t):
        eight = mrow[pl.ds(pl.multiple_of(t * 8, 8), 8), :]
        rows_send[2 * t] = eight[0:4, :].astype(BF16)
        rows_send[2 * t + 1] = eight[4:8, :].astype(BF16)

    @pl.loop(1, N_CTX)
    def _(d):
        remote(
            rows_send.at[other(d)], rows_in.at[ctx], rw_ss.at[d], rw_rs.at[d], {"ctx": other(d), "tp": z}
        ).start()

    rows_in[ctx] = rows_send[ctx]

    for n in range(40):
        colsend[n * 128 : (n + 1) * 128, :] = perm[:, n * 128 : (n + 1) * 128].T

    def col_block(c):
        return colsend.at[pl.ds(pl.multiple_of(c * ROWS_W, 32), ROWS_W), :]

    @pl.loop(1, N_CTX)
    def _(d):
        remote(
            col_block(other(d)), colin.at[ctx], co_ss.at[d], co_rs.at[d], {"ctx": other(d), "tp": z}
        ).start()

    colin[ctx] = colsend[pl.ds(pl.multiple_of(ctx * ROWS_W, 32), ROWS_W), :]

    @pl.loop(1, N_CTX)
    def _(d):
        remote(
            idx_send.at[other(d)], idx_in.at[behind(d)], ix_ss.at[d], ix_rs.at[d], {"ctx": other(d), "tp": z}
        ).wait()

    load_text.wait()
    load_cot.wait()
    at_row = (jnp.sum(idx_in[...], axis=0) - 1)[0:1, :]
    at_col = jnp.broadcast_to(at_row, (SLOTS, SLOTS)).T
    for b in range(8):
        drow[:, 128 * b : 128 * (b + 1)] = jnp.where(
            at_col == iota((SLOTS, SLOTS), 1) + 128 * b, 1.0, 0.0
        ).astype(BF16)

    @pl.loop(0, 4)
    def _(n):
        cols_n = pl.ds(pl.multiple_of(n * 256, 256), 256)
        cotsel[:, cols_n] = dot(drow[...], cot[:, cols_n])

    @pl.loop(1, N_CTX)
    def _(d):
        remote(
            rows_send.at[other(d)], rows_in.at[behind(d)], rw_ss.at[d], rw_rs.at[d], {"ctx": other(d), "tp": z}
        ).wait()

    @pl.loop(0, N_CTX)
    def _(s):
        four = rows_in[s].astype(F32)
        for k in range(4):
            incf[pl.ds(k * N_CTX + s, 1), :] = four[k : k + 1, :]

    gain_row = gain[...].astype(F32)

    @pl.loop(0, 8)
    def _(b):
        rows_b = pl.ds(pl.multiple_of(b * 128, 128), 128)
        placed = jnp.where(iota((128, SLOTS), 0) + 128 * b == at_row, 1.0, 0.0).astype(F32)
        taken = jnp.sum(placed, axis=1, keepdims=True) > 0.0
        vision = dot(placed.astype(BF16), incf[...].astype(BF16))
        sq = jnp.zeros((128, 128), F32)
        inner = jnp.zeros((128, 128), F32)
        for n in range(8):
            cols_n = slice(128 * n, 128 * (n + 1))
            emb = jnp.where(taken, vision[:, cols_n], text[rows_b, cols_n].astype(F32))
            text[rows_b, cols_n] = emb.astype(BF16)
            sq = sq + emb * emb
            inner = inner + emb * (gain_row[:, cols_n] * cot[rows_b, cols_n].astype(F32))
        stats[z, pl.ds(b, 1), :] = jnp.sum(sq.T, axis=0, keepdims=True)
        stats[z, pl.ds(8 + b, 1), :] = jnp.sum(inner.T, axis=0, keepdims=True)

    def stat_copy(d, slot):
        return remote(
            stats.at[z], stats.at[slot], st_ss.at[d], st_rs.at[d], {"ctx": ctx, "tp": (z + d) % NZ}
        )

    @pl.loop(1, NZ)
    def _(d):
        stat_copy(d, z).start()

    @pl.loop(1, N_CTX)
    def _(d):
        remote(
            col_block(other(d)), colin.at[behind(d)], co_ss.at[d], co_rs.at[d], {"ctx": other(d), "tp": z}
        ).wait()

    @pl.loop(0, N_CTX)
    def _(s):
        rows_s = pl.ds(pl.multiple_of(s * SLOTS, 128), SLOTS)
        came = colin[s].astype(F32)
        colf[rows_s, :] = came[0:128, :].T
        colg[rows_s, :] = jnp.concatenate([came[128:160, :], jnp.zeros((96, 128), F32)], axis=0).T

    @pl.loop(1, NZ)
    def _(d):
        stat_copy(d, (z + NZ - d) % NZ).wait()

    total = jnp.sum(stats[...], axis=0)
    scale = lax.rsqrt(total[0:8, :] / D + 1e-06)
    inner_all = total[8:16, :]
    scale_at = jnp.zeros((1, SLOTS), F32)
    inner_at = jnp.zeros((1, SLOTS), F32)
    for b in range(8):
        here = iota((128, SLOTS), 0) + 128 * b == at_row
        scale_b = jnp.broadcast_to(scale[b : b + 1, :], (128, 128)).T
        inner_b = jnp.broadcast_to(inner_all[b : b + 1, :], (128, 128)).T
        scol[128 * b : 128 * (b + 1), :] = scale_b
        scale_at = scale_at + jnp.sum(jnp.where(here, scale_b, 0.0), axis=0, keepdims=True)
        inner_at = inner_at + jnp.sum(jnp.where(here, inner_b, 0.0), axis=0, keepdims=True)
    s_at = jnp.broadcast_to(scale_at, (SLOTS, SLOTS)).T
    i_at = jnp.broadcast_to(inner_at, (SLOTS, SLOTS)).T
    own_g = pl.ds(pl.multiple_of(ctx * SLOTS, 128), SLOTS)
    for n in range(8):
        cols_n = slice(128 * n, 128 * (n + 1))
        gained = gain_row[:, cols_n] * cotsel[:, cols_n]
        gf[own_g, cols_n] = (s_at * gained - incf[:, cols_n] * (s_at * s_at * s_at) * i_at / D).astype(BF16)

    gg = PlaneGather(p, gf, SLOTS, g_ss, g_rs)
    gg.start()

    def normed_copy(b):
        rows_b = pl.ds(pl.multiple_of(b * 256, 256), 256)
        return pltpu.make_async_copy(normed.at[rows_b, :], normed_out.at[rows_b, :], local.at[4 + b])

    def normed_block(b):
        for h in range(2):
            rows_b = pl.ds(b * 256 + h * 128, 128)
            for n in range(8):
                cols_n = slice(128 * n, 128 * (n + 1))
                normed[rows_b, cols_n] = (
                    text[rows_b, cols_n].astype(F32) * scol[rows_b, :] * gain_row[:, cols_n]
                ).astype(BF16)
        normed_copy(b).start()

    def order_block(t):
        for k in range(4):
            rows_k = pl.ds(pl.multiple_of(t * SLOTS + k * N_CTX, 32), N_CTX)
            every = pl.ds(t * 4 + k, N_CTX, stride=SLOTS)
            cols[rows_k, 0:128] = colf[every, :].astype(BF16)
            cols[rows_k, 128:160] = colg[every, :][:, 0:32].astype(BF16)

    def add_pair(i, j, first=False):
        base = gg.pair_rows(i, j)
        rows_p = pl.ds(pl.multiple_of(base, 256), 256)
        part = lax.dot_general(
            cols[rows_p, :], gf[rows_p, :], (((0,), (0,)), ((), ())), preferred_element_type=F32
        )
        grad_out[...] = part if first else grad_out[...] + part

    normed_block(0)
    normed_block(1)
    gg.first()
    normed_block(2)
    normed_block(3)
    gg.second()

    @pl.loop(0, N_CTX)
    def _(t):
        order_block(t)

    gg.third(0)
    gg.from_sibling(0, 0)
    add_pair(0, 0, True)
    gg.third(1)
    for i, j in ((1, 0), (0, 1)):
        gg.from_sibling(i, j)
        add_pair(i, j)
    gg.third(2)
    for i, j in ((2, 0), (0, 2)):
        gg.from_sibling(i, j)
        add_pair(i, j)
    gg.third(3)
    for i, j in ((1, 1), (1, 2), (2, 1), (2, 2)):
        gg.from_sibling(i, j)
        add_pair(i, j)
    gg.fourth(0)
    gg.fourth(1)
    for i, j in ((3, 0), (0, 3), (3, 1), (1, 3)):
        gg.from_sibling(i, j)
        add_pair(i, j)
    gg.fourth(2)
    for i, j in ((3, 2), (2, 3)):
        gg.from_sibling(i, j)
        add_pair(i, j)
    gg.fourth(3)
    gg.from_sibling(3, 3)
    add_pair(3, 3)

    for b in range(4):
        normed_copy(b).wait()
    for c in (wg, gg, og, ag):
        c.finish()
    for c in osib:
        c.wait_send()


def shards(
    patches,
    window_ids,
    positions,
    text_embed,
    cotangent,
    qkv_weight,
    out_weight,
    merger_weight,
    norm_gain,
):
    vmem = pl.BlockSpec(memory_space=pltpu.VMEM)
    anywhere = pl.BlockSpec(memory_space=pl.ANY)
    dma = pltpu.SemaphoreType.DMA
    return pl.pallas_call(
        kernel,
        out_shape=(
            jax.ShapeDtypeStruct((TOK, 1024), BF16),
            jax.ShapeDtypeStruct((ROWS_W, 1024), F32),
        ),
        in_specs=[vmem, vmem, vmem, anywhere, anywhere, vmem, anywhere, anywhere, vmem],
        out_specs=(anywhere, vmem),
        scratch_shapes=[
            pltpu.VMEM((N_CTX * ROWS_W, 1024), BF16),
            pltpu.VMEM((N_CTX * SLOTS, 1024), BF16),
            pltpu.VMEM((DV, DV), BF16),
            pltpu.VMEM((DV, 512), BF16),
            pltpu.VMEM((512, DV), BF16),
            pltpu.VMEM((512, DV), BF16),
            pltpu.VMEM((SLOTS, 4 * DV), BF16),
            pltpu.VMEM((4 * DV, SLOTS), BF16),
            pltpu.VMEM((N_CTX, ROWS_W, SLOTS), BF16),
            pltpu.VMEM((N_CTX * SLOTS, 128), F32),
            pltpu.VMEM((N_CTX * SLOTS, 128), F32),
            pltpu.VMEM((N_CTX * SLOTS, ROWS_W), BF16),
            pltpu.VMEM((TOK, 1024), BF16),
            pltpu.VMEM((TOK, 1024), BF16),
            pltpu.VMEM((TOK, 1024), BF16),
            pltpu.VMEM((512, HCOLS), BF16),
            pltpu.VMEM((512, HCOLS), BF16),
            pltpu.VMEM((512, HCOLS), BF16),
            pltpu.VMEM((HCOLS, 512), BF16),
            pltpu.VMEM((512, 128), jnp.int32),
            pltpu.VMEM((SLOTS, 1024), F32),
            pltpu.VMEM((N_CTX, 4, 1024), BF16),
            pltpu.VMEM((N_CTX, 4, 1024), BF16),
            pltpu.VMEM((SLOTS, 1024), F32),
            pltpu.VMEM((N_CTX, 8, SLOTS), jnp.int32),
            pltpu.VMEM((N_CTX, 8, SLOTS), jnp.int32),
            pltpu.VMEM((NZ, 16, SLOTS), F32),
            pltpu.VMEM((SLOTS, 1024), F32),
            pltpu.VMEM((TOK, SLOTS), F32),
            pltpu.VMEM((SLOTS, TOK), BF16),
            dma((8,)),
            dma((36,)), dma((36,)), dma((36,)), dma((36,)),
            dma((8,)), dma((8,)), dma((8,)), dma((8,)), dma((8,)), dma((8,)),
            dma((N_CTX,)), dma((N_CTX,)), dma((N_CTX,)), dma((N_CTX,)), dma((N_CTX,)), dma((N_CTX,)),
            dma((NZ,)), dma((NZ,)),
        ],
        compiler_params=pltpu.CompilerParams(
            collective_id=0, has_side_effects=True, vmem_limit_bytes=62 * 1024 * 1024
        ),
    )(
        patches,
        window_ids.reshape(1, -1),
        positions.reshape(1, -1),
        text_embed,
        cotangent,
        qkv_weight,
        out_weight,
        merger_weight,
        norm_gain.reshape(1, -1),
    )


def solution(mesh):
    in_specs = (
        P("ctx", None),
        P("ctx"),
        P("ctx"),
        P("ctx", "tp"),
        P("ctx", "tp"),
        P(None, None, "tp"),
        P("tp", None),
        P("ctx", "tp"),
        P("tp"),
    )
    out_specs = (P("ctx", "tp"), P("ctx", "tp"))
    return jax.shard_map(shards, mesh=mesh, in_specs=in_specs, out_specs=out_specs, check_vma=False)
```

time: 240 us -> 131 us (0.55)
  Pallas kernels: 0 us -> 121 us
  waiting for transfers between devices: 110 us -> 0 us
  matrix products: 32.1 us -> 0 us
  blocking collectives: 28.8 us -> 0 us
  starting transfers between devices: 24.6 us -> 0 us
  between operations: 15.8 us -> 0.65 us
  local copies, waits for them, and re-layouts: 21.8 us -> 8.87 us
  other arithmetic: 6.13 us -> 0 us
    pallas_call x0 -> x1, Pallas kernels: none -> 121 us  [shards(): pl.pallas_call(kernel, out_shape=(jax.ShapeDtypeStruct((TOK, 1024), BF16)...]
    psum x1 -> x0, waiting for transfers between devices: 66.8 us -> none  [shards(): lax.psum(partial_out.astype(jnp.bfloat16), 'tp').astype(jnp.float32)]
    dot_general x10 -> x0, matrix products: 31.1 us -> none  [the longest x3 11.4 us: contract_rows(): lax.dot_general(left, right, (((0,), (0,)), ((), ())), preferred_element_...]
    all_to_all x2 -> x0, blocking collectives: 28.8 us -> none  [the longest x1 17.6 us: shards(): lax.all_to_all(back_rows, 'ctx', split_axis=0, concat_axis=0, tiled=True)]
    all_gather x2 -> x0, waiting for transfers between devices: 27.4 us -> none  [the longest x1 27.4 us: shards(): lax.all_gather(d_merged, 'ctx', axis=0, tiled=True)]
    all_to_all x3 -> x0, starting transfers between devices: 24.5 us -> none  [the longest x1 11.4 us: shards(): lax.all_to_all(outgoing, 'ctx', split_axis=0, concat_axis=0, tiled=True)]
    all_to_all x3 -> x0, waiting for transfers between devices: 15.3 us -> none  [the longest x1 15.3 us: shards(): lax.all_to_all(merged_in, 'ctx', split_axis=1, concat_axis=0, tiled=True)]
    all_to_all x7 -> x0, local copies, waits for them, and re-layouts: 9.58 us -> none  [the longest x2 8.02 us: shards(): lax.all_to_all(merged_in, 'ctx', split_axis=1, concat_axis=0, tiled=True)]
  transfers between devices with their start and end apart: 6 -> 0, of which waited for: 3 -> 0; matrix products, arithmetic and copies ran while one was open for 12% -> 0% of each run, Pallas kernels for 0% -> 0%
where the time goes in v1:
time: 131 us; the launch traced here: 130 us
  Pallas kernels  121 us (92%)
  local copies, waits for them, and re-layouts  8.87 us (7%)
    pallas_call x1, Pallas kernels, shards(): pl.pallas_call(kernel, out_shape=(jax.ShapeDtypeStruct((TOK, 1024), BF16)...  121 us
    unnamed x5, local copies, waits for them, and re-layouts  7.59 us

profile of v1, /device:TPU:1, one launch (start us, length us, event | category | flops | bytes accessed | tf_op | source)
XLA Modules:
  0.0 130.5 jit_solution(7726256049791120173)
XLA Ops:
  0.6 1.3 reshape.15.gain
  1.9 3.6 %copy.11.qkv = bf16[3,1280,160]{2,1,0:T(8,128)(2,1)} copy(bf16[3,1280,160]{1,2,0:T(8,128)(2,1)} %param.14) | data formatting | bytes 2457600 | tf_op args[5]
  5.5 121.0 %shard_map.104 = (bf16[1024,1024]{1,0:T(8,128)(2,1)}, f32[160,1024]{1,0:T(8,128)}) custom-call(bf16[512,1280]{1,0:T(8,128)(2,1)} %pat.1, s32[1,512]{1,0:T(1,128)} %bitcast.2, s32[1,128]{1,0:T(1,128)} %bitcast.3, bf16[1024,1024]{1,0:T(8,128)(2,1)} %text_in.1, bf16[1024,1024]{1,0:T(8,128)(2,1)} %cot_in.1, bf16[3,1280,160]{2,1,0:T(8,128)(2,1)} %copy.11.qkv, ...), custom_call_target="tpu_custom_call" | custom-call | tf_op jit(solution)/shard_map/pallas_call | solution.py:582
  126.5 0.0 copy-start
  126.5 3.1 %copy.14 = bf16[1024,1024]{1,0:T(8,128)(2,1)} copy(bf16[1024,1024]{1,0:T(8,128)(2,1)} %get-tuple-element.4) | data formatting | bytes 4194304
  129.6 0.0 copy-done
  129.6 0.8 copy.15
Async XLA Ops:
  126.5 3.2 %copy-start = (f32[160,1024]{1,0:T(8,128)S(1)}, f32[160,1024]{1,0:T(8,128)}, u32[]{:S(2)}) copy-start(f32[160,1024]{1,0:T(8,128)} %get-tuple-element.5) | copy-start | bytes 1966084

commit v2 on v1

--- a/solution.py
+++ b/solution.py
@@ -88,19 +88,21 @@
 
     def item(self, i):
         o = self.p.offs
+        if i:
+            self.sibling(i, 0)
         self.send(4 + 4 * i, self.block(o[i], 0), self.p.dev(0, 1))
         self.send(5 + 4 * i, self.block(o[i], 0), self.p.dev(0, 3))
-        self.sibling(i, 0)
 
     def start(self):
         own = self.block(0, 0)
         self.send(0, own, self.p.dev(1, 0))
         self.send(1, own, self.p.dev(3, 0))
-        self.item(0)
+        self.sibling(0, 0)
 
     def first(self):
         self.recv(0, self.block(3, 0))
         self.send(2, self.block(3, 0, 0), self.p.dev(1, 0))
+        self.item(0)
         self.item(1)
         self.recv(1, self.block(1, 0))
         self.send(3, self.block(1, 0, 1), self.p.dev(3, 0))
@@ -146,29 +148,24 @@
         self.p, self.region, self.ss, self.rs = place, region, ss, rs
         self.started = []
 
+    def copy(self, s, way):
+        part = way if s == 4 else None
+        src = (s - 1, (NZ + 1 - s) % NZ)[way]
+        dst = (s, NZ - s)[way]
+        return remote(
+            self.region(src, part), self.region(dst, part), self.ss.at[4 * way + s - 1], self.rs.at[4 * way + s - 1],
+            {"ctx": self.p.ctx, "tp": (self.p.z + (1, NZ - 1)[way]) % NZ},
+        )
+
     def step(self, s):
-        z = self.p.z
         for way in range(2):
-            sign = 1 - 2 * way
-            part = way if s == 4 else None
-            src = self.region((z - sign * (s - 1) + NZ) % NZ, part)
-            c = remote(
-                src, src, self.ss.at[4 * way + s - 1], self.rs.at[4 * way + s - 1],
-                {"ctx": self.p.ctx, "tp": (z + sign + NZ) % NZ},
-            )
+            c = self.copy(s, way)
             c.start()
             self.started.append(c)
 
     def recv(self, s):
-        z = self.p.z
         for way in range(2):
-            sign = 1 - 2 * way
-            part = way if s == 4 else None
-            dst = self.region((z - sign * s + NZ) % NZ, part)
-            remote(
-                dst, dst, self.ss.at[4 * way + s - 1], self.rs.at[4 * way + s - 1],
-                {"ctx": self.p.ctx, "tp": (z + sign + NZ) % NZ},
-            ).wait_recv()
+            self.copy(s, way).wait_recv()
 
     def finish(self):
         for c in self.started:
@@ -176,12 +173,12 @@
 
 
 def kernel(
-    pat, wid, pos, text_in, cot_in, qkv, ow_in, w_in, gain,
+    pat_in, wid, pos, text_in, cot_in, qkv_in, ow_in, w_in, gain,
     normed_out, grad_out,
-    wf, gf, owf, attf, att_t, hid, perm, colsend, colin, colf, colg, cols, text, cot, normed,
+    pat, qkv, wf, gf, owf, attf, att_t, att_u, hacc, hid, perm, colsend, colin, colf, colg, cols, text, cot, normed,
     q0s, q1s, ks, vts, widc, mrow, rows_send, rows_in, incf, idx_send, idx_in, stats, cotsel, scol, drow,
     local, w_ss, w_rs, g_ss, g_rs, ow_ss, ow_rs, osib_ss, osib_rs, at_ss, at_rs,
-    ix_ss, ix_rs, rw_ss, rw_rs, co_ss, co_rs, st_ss, st_rs,
+    ix_ss, ix_rs, rw_ss, rw_rs, co_ss, co_rs, cg_ss, cg_rs, st_ss, st_rs,
 ):
     p = Place()
     ctx, z, core = p.ctx, p.z, p.core
@@ -192,6 +189,24 @@
     def behind(d):
         return (ctx + N_CTX - d) % N_CTX
 
+    scope = []
+
+    def mark(name):
+        if scope:
+            scope.pop().__exit__(None, None, None)
+        if name:
+            scope.append(jax.named_scope(name))
+            scope[-1].__enter__()
+
+    mark("index")
+    load_pat = pltpu.make_async_copy(pat_in, pat, local.at[8])
+    load_qkv = pltpu.make_async_copy(qkv_in, qkv, local.at[9])
+    load_pat.start()
+    load_qkv.start()
+
+    def block160(ref, c):
+        return ref.at[pl.ds(pl.multiple_of(c * ROWS_W, 32), ROWS_W), :]
+
     barrier = pltpu.get_barrier_semaphore()
 
     @pl.loop(1, N_CTX)
@@ -203,7 +218,7 @@
         pl.semaphore_signal(barrier, inc=1, device_id={"ctx": ctx, "tp": (z + d) % NZ}, device_id_type=MESH)
 
     own_w = wf.at[pl.ds(pl.multiple_of(ctx * ROWS_W, 32), ROWS_W), :]
-    own_ow = owf.at[pl.ds(pl.multiple_of(z * HCOLS, 32), HCOLS), :]
+    own_ow = owf.at[pl.ds(0, HCOLS), :]
     load_w = pltpu.make_async_copy(w_in, own_w, local.at[0])
     load_ow = pltpu.make_async_copy(ow_in, own_ow, local.at[1])
     load_text = pltpu.make_async_copy(text_in, text, local.at[2])
@@ -238,51 +253,17 @@
     for b in range(4):
         widc[128 * b : 128 * (b + 1), :] = jnp.broadcast_to(wid[:, 128 * b : 128 * (b + 1)], (128, 128)).T
 
-    pl.semaphore_wait(barrier, N_CTX - 1 + NZ - 1)
-
-    wg = PlaneGather(p, wf, ROWS_W, w_ss, w_rs)
-    load_w.wait()
-    wg.start()
-
-    def ow_region(zz, part):
-        base = pl.multiple_of(zz * HCOLS + core * 80, 16)
-        if part is None:
-            return owf.at[pl.ds(base, 80), :]
-        return owf.at[pl.ds(base, 80), pl.ds(part * 640, 640)]
-
-    def att_region(zz, part):
-        if part is None:
-            return attf.at[pl.ds(pl.multiple_of(zz * HCOLS, 32), HCOLS), :]
-        return attf.at[pl.ds(pl.multiple_of(zz * HCOLS + part * 80, 16), 80), :]
-
-    osib = []
-
-    def ow_to_sibling(k, zz):
-        src = ow_region(zz, None)
-        c = remote(src, src, osib_ss.at[k], osib_rs.at[k], {"ctx": p.sib, "tp": z})
-        c.start()
-        osib.append(c)
-
-    og = Ring(p, ow_region, ow_ss, ow_rs)
-    ag = Ring(p, att_region, at_ss, at_rs)
-    load_ow.wait()
-    og.step(1)
-
-    @pl.loop(1, N_CTX)
-    def _(d):
-        remote(
-            idx_send.at[other(d)], idx_in.at[ctx], ix_ss.at[d], ix_rs.at[d], {"ctx": other(d), "tp": z}
-        ).start()
-
+    mark("qkv")
+    load_pat.wait()
+    load_qkv.wait()
     patches = pat[...]
     lane = iota((512, HCOLS), 1)
-    q = dot(patches, qkv[0]).astype(BF16).astype(F32)
+    q = dot_nt(patches, qkv[0]).astype(BF16).astype(F32)
     q0s[...] = jnp.where(lane < HEAD_DIM, q, 0.0).astype(BF16)
     q1s[...] = jnp.where(lane < HEAD_DIM, 0.0, q).astype(BF16)
-    ks[...] = dot(patches, qkv[1]).astype(BF16)
-    vts[...] = dot(patches, qkv[2]).astype(BF16).T
-    wg.first()
-
+    ks[...] = dot_nt(patches, qkv[1]).astype(BF16)
+    vts[...] = dot_nt(qkv[2], patches).astype(BF16)
+    mark("attend")
     factor = 1.0 / HEAD_DIM**0.5
 
     @pl.loop(0, 4)
@@ -298,50 +279,123 @@
             probs = (weights / jnp.sum(weights, axis=0, keepdims=True)).astype(BF16)
             parts.append(dot(vts[...], probs))
         row = iota((HCOLS, 128), 0)
-        attf[pl.ds(pl.multiple_of(z * HCOLS, 32), HCOLS), cols_b] = jnp.where(
+        attf[0:HCOLS, cols_b] = jnp.where(
             row < HEAD_DIM, parts[0], parts[1]
         ).astype(BF16)
 
+    mark("barrier")
+    pl.semaphore_wait(barrier, N_CTX - 1 + NZ - 1)
+
+    wg = PlaneGather(p, wf, ROWS_W, w_ss, w_rs)
+    load_w.wait()
+    wg.start()
+
+    def place_of(r):
+        return r if r < 4 else 7 if r == 4 else r - 1
+
+    def ow_region(r, part):
+        base = pl.multiple_of(place_of(r) * HCOLS + core * 80, 16)
+        if part is None:
+            return owf.at[pl.ds(base, 80), :]
+        return owf.at[pl.ds(base, 80), pl.ds(part * 640, 640)]
+
+    def att_region(r, part):
+        if part is None:
+            return attf.at[pl.ds(place_of(r) * HCOLS, HCOLS), :]
+        return attf.at[pl.ds(place_of(r) * HCOLS + part * 80, 80), :]
+
+    osib = []
+
+    def ow_to_sibling(r):
+        src = ow_region(r, None)
+        c = remote(src, src, osib_ss.at[r], osib_rs.at[r], {"ctx": p.sib, "tp": z})
+        c.start()
+        osib.append(c)
+
+    def ow_from_sibling(r):
+        dst = owf.at[pl.ds(pl.multiple_of(place_of(r) * HCOLS + (1 - core) * 80, 16), 80), :]
+        remote(dst, dst, osib_ss.at[r], osib_rs.at[r], {"ctx": p.sib, "tp": z}).wait_recv()
+
+    og = Ring(p, ow_region, ow_ss, ow_rs)
+    ag = Ring(p, att_region, at_ss, at_rs)
+    load_ow.wait()
+    og.step(1)
     ag.step(1)
 
-    wg.second()
+    mark("w_first")
+    wg.first()
+    mark("ow1")
     og.recv(1)
     og.step(2)
-    wg.third(0)
+    mark("at1")
     ag.recv(1)
     ag.step(2)
+
+    @pl.loop(1, N_CTX)
+    def _(d):
+        remote(
+            idx_send.at[other(d)], idx_in.at[ctx], ix_ss.at[d], ix_rs.at[d], {"ctx": other(d), "tp": z}
+        ).start()
+
+    mark("w_second")
+    wg.second()
+    mark("w30")
+    wg.third(0)
+    mark("ow2")
     og.recv(2)
     og.step(3)
+    mark("w31")
     wg.third(1)
-    wg.third(2)
+    mark("at2")
     ag.recv(2)
     ag.step(3)
+    mark("w32")
+    wg.third(2)
+    mark("ow3")
     og.recv(3)
     og.step(4)
+    for r in (1, 7, 2, 6, 3, 5):
+        ow_to_sibling(r)
+    mark("w33")
     wg.third(3)
+    mark("w40")
+    wg.fourth(0)
+    mark("at3")
     ag.recv(3)
     ag.step(4)
-    for k in (0, 1, 2, 4, 5, 6):
-        ow_to_sibling(k, (z + 5 + k) % NZ)
-    for i in range(4):
-        wg.fourth(i)
+    mark("w41")
+    wg.fourth(1)
+    mark("ow4")
     og.recv(4)
-    ow_to_sibling(7, (z + 4) % NZ)
-    ag.recv(4)
-    for k in (0, 1, 2, 4, 5, 6, 7):
-        zz = (z + 5 + k) % NZ if k < 7 else (z + 4) % NZ
-        dst = owf.at[pl.ds(pl.multiple_of(zz * HCOLS + (1 - core) * 80, 16), 80), :]
-        remote(dst, dst, osib_ss.at[k], osib_rs.at[k], {"ctx": p.sib, "tp": z}).wait_recv()
-
-    for zz in range(NZ):
-        att_t[:, zz * HCOLS : (zz + 1) * HCOLS] = attf[zz * HCOLS : (zz + 1) * HCOLS, :].T
+    ow_to_sibling(4)
+    mark("transpose")
+    for r in range(7):
+        att_t[:, r * HCOLS : (r + 1) * HCOLS] = attf[r * HCOLS : (r + 1) * HCOLS, :].T
+    mark("ow_sib")
+    for r in (1, 7, 2, 6, 3, 5):
+        ow_from_sibling(r)
+    mark("out_proj")
 
     @pl.loop(0, 5)
     def _(n):
         cols_n = pl.ds(pl.multiple_of(n * 256, 256), 256)
-        out = dot(att_t[...], owf[:, cols_n])
-        hid[:, cols_n] = (pat[:, cols_n].astype(F32) + out).astype(BF16)
-
+        hacc[:, cols_n] = pat[:, cols_n].astype(F32) + dot(att_t[...], owf[0 : 7 * HCOLS, cols_n])
+
+    mark("w42")
+    wg.fourth(2)
+    wg.fourth(3)
+    mark("at4")
+    ag.recv(4)
+    ow_from_sibling(4)
+    mark("hidden")
+    att_u[...] = attf[7 * HCOLS : 8 * HCOLS, :].T
+
+    @pl.loop(0, 5)
+    def _(n):
+        cols_n = pl.ds(pl.multiple_of(n * 256, 256), 256)
+        hid[:, cols_n] = (hacc[:, cols_n] + dot(att_u[...], owf[7 * HCOLS : 8 * HCOLS, cols_n])).astype(BF16)
+
+    mark("perm")
     spread_at = jnp.where(iota((SLOTS, 512), 0) == iota((SLOTS, 512), 1) // 4, 1.0, 0.0).astype(BF16)
     bucket512 = dot(jnp.broadcast_to(bucket_row, (8, SLOTS)).astype(BF16), spread_at)[0:1, :]
     chosen = iota((SLOTS, 512), 0).astype(F32) == bucket512
@@ -352,15 +406,18 @@
                 select, hid[:, n * 256 : (n + 1) * 256]
             ).astype(BF16)
 
+    mark("w_sib")
     for i in range(4):
         for j in range(4):
             wg.from_sibling(i, j)
 
+    mark("merge")
     @pl.loop(0, 4)
     def _(n):
         cols_n = pl.ds(pl.multiple_of(n * 256, 256), 256)
         mrow[:, cols_n] = dot(perm[...], wf[:, cols_n]).astype(BF16).astype(F32)
 
+    mark("rows_send")
     @pl.loop(0, N_CTX // 2)
     def _(t):
         eight = mrow[pl.ds(pl.multiple_of(t * 8, 8), 8), :]
@@ -375,26 +432,38 @@
 
     rows_in[ctx] = rows_send[ctx]
 
-    for n in range(40):
-        colsend[n * 128 : (n + 1) * 128, :] = perm[:, n * 128 : (n + 1) * 128].T
-
-    def col_block(c):
-        return colsend.at[pl.ds(pl.multiple_of(c * ROWS_W, 32), ROWS_W), :]
-
-    @pl.loop(1, N_CTX)
-    def _(d):
-        remote(
-            col_block(other(d)), colin.at[ctx], co_ss.at[d], co_rs.at[d], {"ctx": other(d), "tp": z}
-        ).start()
-
-    colin[ctx] = colsend[pl.ds(pl.multiple_of(ctx * ROWS_W, 32), ROWS_W), :]
-
+    mark("colsend")
+
+    def source(zz, x):
+        return (x * NY + (x + zz) % NY) * 2 + zz // NY
+
+    x_here = ctx // (2 * NY)
+    turn = ctx == source(z, x_here)
+
+    @pl.when(turn)
+    def _():
+        for n in range(40):
+            colsend[n * 128 : (n + 1) * 128, :] = perm[:, n * 128 : (n + 1) * 128].T
+
+        @pl.loop(1, N_CTX)
+        def _(d):
+            remote(
+                block160(colsend, other(d)), block160(colin, x_here), co_ss.at[d], co_rs.at[x_here],
+                {"ctx": other(d), "tp": z},
+            ).start()
+
+        colin[pl.ds(pl.multiple_of(x_here * ROWS_W, 32), ROWS_W), :] = colsend[
+            pl.ds(pl.multiple_of(ctx * ROWS_W, 32), ROWS_W), :
+        ]
+
+    mark("idx_wait")
     @pl.loop(1, N_CTX)
     def _(d):
         remote(
             idx_send.at[other(d)], idx_in.at[behind(d)], ix_ss.at[d], ix_rs.at[d], {"ctx": other(d), "tp": z}
         ).wait()
 
+    mark("cotsel")
     load_text.wait()
     load_cot.wait()
     at_row = (jnp.sum(idx_in[...], axis=0) - 1)[0:1, :]
@@ -409,63 +478,90 @@
         cols_n = pl.ds(pl.multiple_of(n * 256, 256), 256)
         cotsel[:, cols_n] = dot(drow[...], cot[:, cols_n])
 
+    gains = gain[...].astype(F32)
+
+    def gain_of(n):
+        return gains[n : n + 1, :]
+
+    def row_sums(rows, cots):
+        sq = jnp.zeros((128, 128), F32)
+        inner = jnp.zeros((128, 128), F32)
+        for n in range(8):
+            cols_n = slice(128 * n, 128 * (n + 1))
+            x = rows(cols_n)
+            sq = sq + x * x
+            inner = inner + x * (gain_of(n) * cots(cols_n))
+        return jnp.sum(sq.T, axis=0, keepdims=True), jnp.sum(inner.T, axis=0, keepdims=True)
+
+    mark("text_sums")
+
+    @pl.loop(0, 8)
+    def _(b):
+        rows_b = pl.ds(pl.multiple_of(b * 128, 128), 128)
+        sq, inner = row_sums(
+            lambda c: text[rows_b, c].astype(F32), lambda c: cot[rows_b, c].astype(F32)
+        )
+        stats[z, pl.ds(b, 1), :] = sq
+        stats[z, pl.ds(8 + b, 1), :] = inner
+
+    mark("rows_wait")
+
     @pl.loop(1, N_CTX)
     def _(d):
         remote(
             rows_send.at[other(d)], rows_in.at[behind(d)], rw_ss.at[d], rw_rs.at[d], {"ctx": other(d), "tp": z}
         ).wait()
 
-    @pl.loop(0, N_CTX)
+    mark("embed")
+
+    @pl.loop(0, N_CTX, unroll=4)
     def _(s):
         four = rows_in[s].astype(F32)
         for k in range(4):
             incf[pl.ds(k * N_CTX + s, 1), :] = four[k : k + 1, :]
 
-    gain_row = gain[...].astype(F32)
+    mark("new_sums")
+    sq_new, inner_new = row_sums(lambda c: incf[:, c], lambda c: cotsel[:, c])
+    sq_new = jnp.broadcast_to(sq_new, (SLOTS, SLOTS)).T
+    inner_new = jnp.broadcast_to(inner_new, (SLOTS, SLOTS)).T
+    for b in range(8):
+        here = at_col == iota((SLOTS, SLOTS), 1) + 128 * b
+        taken = jnp.sum(jnp.where(here, 1.0, 0.0), axis=0, keepdims=True) > 0.0
+        for base, new in ((b, sq_new), (8 + b, inner_new)):
+            put = jnp.sum(jnp.where(here, new, 0.0), axis=0, keepdims=True)
+            stats[z, base : base + 1, :] = jnp.where(taken, put, stats[z, base : base + 1, :])
+
+    def stat_copy(d, slot):
+        return remote(
+            stats.at[z], stats.at[slot], st_ss.at[d], st_rs.at[d], {"ctx": ctx, "tp": (z + d) % NZ}
+        )
+
+    mark("stat")
+
+    @pl.loop(1, NZ)
+    def _(d):
+        stat_copy(d, z).start()
+
+    mark("place")
+    inc = incf[...].astype(BF16)
 
     @pl.loop(0, 8)
     def _(b):
         rows_b = pl.ds(pl.multiple_of(b * 128, 128), 128)
         placed = jnp.where(iota((128, SLOTS), 0) + 128 * b == at_row, 1.0, 0.0).astype(F32)
         taken = jnp.sum(placed, axis=1, keepdims=True) > 0.0
-        vision = dot(placed.astype(BF16), incf[...].astype(BF16))
-        sq = jnp.zeros((128, 128), F32)
-        inner = jnp.zeros((128, 128), F32)
+        vision = dot(placed.astype(BF16), inc)
         for n in range(8):
             cols_n = slice(128 * n, 128 * (n + 1))
-            emb = jnp.where(taken, vision[:, cols_n], text[rows_b, cols_n].astype(F32))
-            text[rows_b, cols_n] = emb.astype(BF16)
-            sq = sq + emb * emb
-            inner = inner + emb * (gain_row[:, cols_n] * cot[rows_b, cols_n].astype(F32))
-        stats[z, pl.ds(b, 1), :] = jnp.sum(sq.T, axis=0, keepdims=True)
-        stats[z, pl.ds(8 + b, 1), :] = jnp.sum(inner.T, axis=0, keepdims=True)
-
-    def stat_copy(d, slot):
-        return remote(
-            stats.at[z], stats.at[slot], st_ss.at[d], st_rs.at[d], {"ctx": ctx, "tp": (z + d) % NZ}
-        )
-
-    @pl.loop(1, NZ)
-    def _(d):
-        stat_copy(d, z).start()
-
-    @pl.loop(1, N_CTX)
-    def _(d):
-        remote(
-            col_block(other(d)), colin.at[behind(d)], co_ss.at[d], co_rs.at[d], {"ctx": other(d), "tp": z}
-        ).wait()
-
-    @pl.loop(0, N_CTX)
-    def _(s):
-        rows_s = pl.ds(pl.multiple_of(s * SLOTS, 128), SLOTS)
-        came = colin[s].astype(F32)
-        colf[rows_s, :] = came[0:128, :].T
-        colg[rows_s, :] = jnp.concatenate([came[128:160, :], jnp.zeros((96, 128), F32)], axis=0).T
+            text[rows_b, cols_n] = jnp.where(taken, vision[:, cols_n].astype(BF16), text[rows_b, cols_n])
+
+    mark("stat_wait")
 
     @pl.loop(1, NZ)
     def _(d):
         stat_copy(d, (z + NZ - d) % NZ).wait()
 
+    mark("drows")
     total = jnp.sum(stats[...], axis=0)
     scale = lax.rsqrt(total[0:8, :] / D + 1e-06)
     inner_all = total[8:16, :]
@@ -483,7 +579,7 @@
     own_g = pl.ds(pl.multiple_of(ctx * SLOTS, 128), SLOTS)
     for n in range(8):
         cols_n = slice(128 * n, 128 * (n + 1))
-        gained = gain_row[:, cols_n] * cotsel[:, cols_n]
+        gained = gain_of(n) * cotsel[:, cols_n]
         gf[own_g, cols_n] = (s_at * gained - incf[:, cols_n] * (s_at * s_at * s_at) * i_at / D).astype(BF16)
 
     gg = PlaneGather(p, gf, SLOTS, g_ss, g_rs)
@@ -499,7 +595,7 @@
             for n in range(8):
                 cols_n = slice(128 * n, 128 * (n + 1))
                 normed[rows_b, cols_n] = (
-                    text[rows_b, cols_n].astype(F32) * scol[rows_b, :] * gain_row[:, cols_n]
+                    text[rows_b, cols_n].astype(F32) * scol[rows_b, :] * gain_of(n)
                 ).astype(BF16)
         normed_copy(b).start()
 
@@ -518,51 +614,138 @@
         )
         grad_out[...] = part if first else grad_out[...] + part
 
+    def col_region(r, part):
+        if part is None:
+            return colin.at[pl.ds(r * 640, 640), :]
+        return colin.at[pl.ds(r * 640 + part * 320, 320), :]
+
+    cg = Ring(p, col_region, cg_ss, cg_rs)
+
+    def turn_cols(r):
+        @pl.loop(0, 4)
+        def _(x):
+            rows_s = pl.ds(pl.multiple_of(source((z + NZ - r) % NZ, x) * SLOTS, 128), SLOTS)
+            came = colin[pl.ds(pl.multiple_of((r * 4 + x) * ROWS_W, 32), ROWS_W), :].astype(F32)
+            colf[rows_s, :] = came[0:128, :].T
+            colg[rows_s, :] = jnp.concatenate([came[128:160, :], jnp.zeros((96, 128), F32)], axis=0).T
+
+    mark("col_wait")
+    for j in range(4):
+
+        @pl.when(ctx != source(z, j))
+        def _():
+            remote(
+                block160(colsend, ctx), block160(colin, j), co_ss.at[0], co_rs.at[j], {"ctx": p.sib, "tp": z}
+            ).wait_recv()
+
+    cg.step(1)
+    mark("normed")
     normed_block(0)
     normed_block(1)
-    gg.first()
     normed_block(2)
     normed_block(3)
+    turn_cols(0)
+    mark("g1")
+    gg.first()
+    mark("c1")
+    cg.recv(1)
+    cg.step(2)
+    mark("col_t")
+    turn_cols(1)
+    turn_cols(7)
+    mark("g2")
     gg.second()
+    mark("c2")
+    cg.recv(2)
+    cg.step(3)
+    mark("g30")
+    gg.third(0)
+    mark("col_t")
+    turn_cols(2)
+    turn_cols(6)
+    mark("g31")
+    gg.third(1)
+    mark("c3")
+    cg.recv(3)
+    cg.step(4)
+    mark("col_t")
+    turn_cols(3)
+    turn_cols(5)
+    mark("g32")
+    gg.third(2)
+    mark("c4")
+    cg.recv(4)
+    mark("col_t")
+    turn_cols(4)
+    mark("order")
 
     @pl.loop(0, N_CTX)
     def _(t):
         order_block(t)
 
-    gg.third(0)
+    mark("add1")
     gg.from_sibling(0, 0)
     add_pair(0, 0, True)
-    gg.third(1)
     for i, j in ((1, 0), (0, 1)):
         gg.from_sibling(i, j)
         add_pair(i, j)
-    gg.third(2)
     for i, j in ((2, 0), (0, 2)):
         gg.from_sibling(i, j)
         add_pair(i, j)
+    mark("g33")
     gg.third(3)
     for i, j in ((1, 1), (1, 2), (2, 1), (2, 2)):
         gg.from_sibling(i, j)
         add_pair(i, j)
+    mark("g40")
     gg.fourth(0)
     gg.fourth(1)
     for i, j in ((3, 0), (0, 3), (3, 1), (1, 3)):
         gg.from_sibling(i, j)
         add_pair(i, j)
+    mark("g42")
     gg.fourth(2)
     for i, j in ((3, 2), (2, 3)):
         gg.from_sibling(i, j)
         add_pair(i, j)
+    mark("g43")
     gg.fourth(3)
     gg.from_sibling(3, 3)
     add_pair(3, 3)
 
+    mark("end")
     for b in range(4):
         normed_copy(b).wait()
-    for c in (wg, gg, og, ag):
+    for c in (wg, gg, og, ag, cg):
         c.finish()
     for c in osib:
         c.wait_send()
+
+    @pl.when(turn)
+    def _():
+        @pl.loop(1, N_CTX)
+        def _(d):
+            remote(
+                block160(colsend, other(d)), block160(colin, x_here), co_ss.at[d], co_rs.at[0], {"ctx": other(d), "tp": z}
+            ).wait_send()
+
+    mark(None)
+
+
+def hand_out(normed_in, grad_in, normed_out, grad_out, normed, grad, sem_in, sem_out):
+    parts = [
+        (normed_in.at[pl.ds(r, 256), :], normed.at[pl.ds(r, 256), :], normed_out.at[pl.ds(r, 256), :])
+        for r in range(0, TOK, 256)
+    ] + [(grad_in, grad, grad_out)]
+    come = [pltpu.make_async_copy(a, b, sem_in.at[n]) for n, (a, b, _) in enumerate(parts)]
+    go = [pltpu.make_async_copy(b, c, sem_out.at[n]) for n, (_, b, c) in enumerate(parts)]
+    for c in come:
+        c.start()
+    for c, g in zip(come, go):
+        c.wait()
+        g.start()
+    for g in go:
+        g.wait()
 
 
 def shards(
@@ -579,24 +762,28 @@
     vmem = pl.BlockSpec(memory_space=pltpu.VMEM)
     anywhere = pl.BlockSpec(memory_space=pl.ANY)
     dma = pltpu.SemaphoreType.DMA
-    return pl.pallas_call(
+    outs = pl.pallas_call(
         kernel,
         out_shape=(
             jax.ShapeDtypeStruct((TOK, 1024), BF16),
             jax.ShapeDtypeStruct((ROWS_W, 1024), F32),
         ),
-        in_specs=[vmem, vmem, vmem, anywhere, anywhere, vmem, anywhere, anywhere, vmem],
+        in_specs=[anywhere, vmem, vmem, anywhere, anywhere, anywhere, anywhere, anywhere, vmem],
         out_specs=(anywhere, vmem),
         scratch_shapes=[
+            pltpu.VMEM((512, DV), BF16),
+            pltpu.VMEM((3, HCOLS, DV), BF16),
             pltpu.VMEM((N_CTX * ROWS_W, 1024), BF16),
             pltpu.VMEM((N_CTX * SLOTS, 1024), BF16),
             pltpu.VMEM((DV, DV), BF16),
             pltpu.VMEM((DV, 512), BF16),
-            pltpu.VMEM((512, DV), BF16),
+            pltpu.VMEM((512, 7 * HCOLS), BF16),
+            pltpu.VMEM((512, HCOLS), BF16),
+            pltpu.VMEM((512, DV), F32),
             pltpu.VMEM((512, DV), BF16),
             pltpu.VMEM((SLOTS, 4 * DV), BF16),
             pltpu.VMEM((4 * DV, SLOTS), BF16),
-            pltpu.VMEM((N_CTX, ROWS_W, SLOTS), BF16),
+            pltpu.VMEM((N_CTX * ROWS_W, SLOTS), BF16),
             pltpu.VMEM((N_CTX * SLOTS, 128), F32),
             pltpu.VMEM((N_CTX * SLOTS, 128), F32),
             pltpu.VMEM((N_CTX * SLOTS, ROWS_W), BF16),
@@ -618,10 +805,10 @@
             pltpu.VMEM((SLOTS, 1024), F32),
             pltpu.VMEM((TOK, SLOTS), F32),
             pltpu.VMEM((SLOTS, TOK), BF16),
-            dma((8,)),
+            dma((10,)),
             dma((36,)), dma((36,)), dma((36,)), dma((36,)),
             dma((8,)), dma((8,)), dma((8,)), dma((8,)), dma((8,)), dma((8,)),
-            dma((N_CTX,)), dma((N_CTX,)), dma((N_CTX,)), dma((N_CTX,)), dma((N_CTX,)), dma((N_CTX,)),
+            dma((N_CTX,)), dma((N_CTX,)), dma((N_CTX,)), dma((N_CTX,)), dma((N_CTX,)), dma((4,)), dma((8,)), dma((8,)),
             dma((NZ,)), dma((NZ,)),
         ],
         compiler_params=pltpu.CompilerParams(
@@ -633,11 +820,26 @@
         positions.reshape(1, -1),
         text_embed,
         cotangent,
-        qkv_weight,
+        jnp.swapaxes(qkv_weight, 1, 2),
         out_weight,
         merger_weight,
-        norm_gain.reshape(1, -1),
+        norm_gain.reshape(8, 128),
     )
+    return pl.pallas_call(
+        hand_out,
+        out_shape=(
+            jax.ShapeDtypeStruct((TOK, 1024), BF16),
+            jax.ShapeDtypeStruct((ROWS_W, 1024), F32),
+        ),
+        in_specs=[anywhere, anywhere],
+        out_specs=(anywhere, anywhere),
+        scratch_shapes=[
+            pltpu.VMEM((TOK, 1024), BF16),
+            pltpu.VMEM((ROWS_W, 1024), F32),
+            dma((5,)),
+            dma((5,)),
+        ],
+    )(*outs)
 
 
 def solution(mesh):

time: 131 us -> 105 us (0.80)
  Pallas kernels: 121 us -> 104 us
  local copies, waits for them, and re-layouts: 8.87 us -> 0 us
    pallas_call x1, Pallas kernels: 121 us -> 101 us  [shards(): pl.pallas_call(kernel, out_shape=(jax.ShapeDtypeStruct((TOK, 1024), BF16)...]
    unnamed x5 -> x0, local copies, waits for them, and re-layouts: 7.59 us -> none
    pallas_call x0 -> x1, Pallas kernels: none -> 2.65 us  [shards(): pl.pallas_call(hand_out, out_shape=(jax.ShapeDtypeStruct((TOK, 1024), BF1...]
where the time goes in v2:
time: 105 us; the launch traced here: 104 us
  Pallas kernels  104 us (99%)
    pallas_call x1, Pallas kernels, shards(): pl.pallas_call(kernel, out_shape=(jax.ShapeDtypeStruct((TOK, 1024), BF16)...  101 us
    pallas_call x1, Pallas kernels, shards(): pl.pallas_call(hand_out, out_shape=(jax.ShapeDtypeStruct((TOK, 1024), BF1...  2.65 us

profile of v2, /device:TPU:1, one launch (start us, length us, event | category | flops | bytes accessed | tf_op | source)
XLA Modules:
  0.0 104.5 jit_solution(748954057462947146)
XLA Ops:
  0.6 101.2 %shard_map.104 = (bf16[1024,1024]{1,0:T(8,128)(2,1)}, f32[160,1024]{1,0:T(8,128)}) custom-call(bf16[512,1280]{1,0:T(8,128)(2,1)} %pat_in.1, s32[1,512]{1,0:T(1,128)} %bitcast.5, s32[1,128]{1,0:T(1,128)} %bitcast.7, bf16[1024,1024]{1,0:T(8,128)(2,1)} %text_in.1, bf16[1024,1024]{1,0:T(8,128)(2,1)} %cot_in.1, bf16[3,160,1280]{2,1,0:T(8,128)(2,1)} %bitcast.4, ...), custom_call_target="tpu_custom_call" | custom-call | tf_op jit(solution)/shard_map/pallas_call | solution.py:765
  101.8 2.7 %shard_map.105 = (bf16[1024,1024]{1,0:T(8,128)(2,1)}, f32[160,1024]{1,0:T(8,128)}) custom-call(bf16[1024,1024]{1,0:T(8,128)(2,1)} %get-tuple-element.4.normed_in, f32[160,1024]{1,0:T(8,128)} %get-tuple-element.5.grad_in), custom_call_target="tpu_custom_call" | custom-call | tf_op jit(solution)/shard_map/pallas_call | solution.py:828

commit v3 on v2

--- a/solution.py
+++ b/solution.py
@@ -15,6 +15,7 @@
 DV = 1280
 HCOLS = 160
 ROWS_W = 160
+PITCH = 136
 F32 = jnp.float32
 BF16 = jnp.bfloat16
 
@@ -97,12 +98,12 @@
         own = self.block(0, 0)
         self.send(0, own, self.p.dev(1, 0))
         self.send(1, own, self.p.dev(3, 0))
+        self.item(0)
         self.sibling(0, 0)
 
     def first(self):
         self.recv(0, self.block(3, 0))
         self.send(2, self.block(3, 0, 0), self.p.dev(1, 0))
-        self.item(0)
         self.item(1)
         self.recv(1, self.block(1, 0))
         self.send(3, self.block(1, 0, 1), self.p.dev(3, 0))
@@ -263,6 +264,43 @@
     q1s[...] = jnp.where(lane < HEAD_DIM, 0.0, q).astype(BF16)
     ks[...] = dot_nt(patches, qkv[1]).astype(BF16)
     vts[...] = dot_nt(qkv[2], patches).astype(BF16)
+    mark("barrier")
+    pl.semaphore_wait(barrier, N_CTX - 1 + NZ - 1)
+
+    wg = PlaneGather(p, wf, ROWS_W, w_ss, w_rs)
+    load_w.wait()
+    wg.start()
+
+    def place_of(r):
+        return (0, 1, 7, 2, 6, 3, 5, 4).index(r)
+
+    def ow_region(r, part):
+        base = pl.multiple_of(place_of(r) * HCOLS + core * 80, 16)
+        if part is None:
+            return owf.at[pl.ds(base, 80), :]
+        return owf.at[pl.ds(base, 80), pl.ds(part * 640, 640)]
+
+    def att_region(r, part):
+        if part is None:
+            return attf.at[pl.ds(place_of(r) * HCOLS, HCOLS), :]
+        return attf.at[pl.ds(place_of(r) * HCOLS + part * 80, 80), :]
+
+    osib = []
+
+    def ow_to_sibling(r):
+        src = ow_region(r, None)
+        c = remote(src, src, osib_ss.at[r], osib_rs.at[r], {"ctx": p.sib, "tp": z})
+        c.start()
+        osib.append(c)
+
+    def ow_from_sibling(r):
+        dst = owf.at[pl.ds(pl.multiple_of(place_of(r) * HCOLS + (1 - core) * 80, 16), 80), :]
+        remote(dst, dst, osib_ss.at[r], osib_rs.at[r], {"ctx": p.sib, "tp": z}).wait_recv()
+
+    og = Ring(p, ow_region, ow_ss, ow_rs)
+    ag = Ring(p, att_region, at_ss, at_rs)
+    load_ow.wait()
+    og.step(1)
     mark("attend")
     factor = 1.0 / HEAD_DIM**0.5
 
@@ -283,53 +321,35 @@
             row < HEAD_DIM, parts[0], parts[1]
         ).astype(BF16)
 
-    mark("barrier")
-    pl.semaphore_wait(barrier, N_CTX - 1 + NZ - 1)
-
-    wg = PlaneGather(p, wf, ROWS_W, w_ss, w_rs)
-    load_w.wait()
-    wg.start()
-
-    def place_of(r):
-        return r if r < 4 else 7 if r == 4 else r - 1
-
-    def ow_region(r, part):
-        base = pl.multiple_of(place_of(r) * HCOLS + core * 80, 16)
-        if part is None:
-            return owf.at[pl.ds(base, 80), :]
-        return owf.at[pl.ds(base, 80), pl.ds(part * 640, 640)]
-
-    def att_region(r, part):
-        if part is None:
-            return attf.at[pl.ds(place_of(r) * HCOLS, HCOLS), :]
-        return attf.at[pl.ds(place_of(r) * HCOLS + part * 80, 80), :]
-
-    osib = []
-
-    def ow_to_sibling(r):
-        src = ow_region(r, None)
-        c = remote(src, src, osib_ss.at[r], osib_rs.at[r], {"ctx": p.sib, "tp": z})
-        c.start()
-        osib.append(c)
-
-    def ow_from_sibling(r):
-        dst = owf.at[pl.ds(pl.multiple_of(place_of(r) * HCOLS + (1 - core) * 80, 16), 80), :]
-        remote(dst, dst, osib_ss.at[r], osib_rs.at[r], {"ctx": p.sib, "tp": z}).wait_recv()
-
-    og = Ring(p, ow_region, ow_ss, ow_rs)
-    ag = Ring(p, att_region, at_ss, at_rs)
-    load_ow.wait()
-    og.step(1)
     ag.step(1)
 
-    mark("w_first")
-    wg.first()
+    def turn_att(r):
+        k = place_of(r)
+        part = attf[k * HCOLS : (k + 1) * HCOLS, :].T
+        if k < 5:
+            att_t[:, k * HCOLS : (k + 1) * HCOLS] = part
+        else:
+            att_u[:, (k - 5) * HCOLS : (k - 4) * HCOLS] = part
+
+    def near_product(n):
+        cols_n = slice(n * 256, (n + 1) * 256)
+        hacc[:, cols_n] = pat[:, cols_n].astype(F32) + dot(att_t[...], owf[0 : 5 * HCOLS, cols_n])
+
+    turn_att(0)
     mark("ow1")
     og.recv(1)
     og.step(2)
+    ow_to_sibling(1)
+    ow_to_sibling(7)
+    mark("w_first")
+    wg.first()
+    mark("w30")
+    wg.third(0)
     mark("at1")
     ag.recv(1)
     ag.step(2)
+    turn_att(1)
+    turn_att(7)
 
     @pl.loop(1, N_CTX)
     def _(d):
@@ -339,23 +359,30 @@
 
     mark("w_second")
     wg.second()
-    mark("w30")
-    wg.third(0)
     mark("ow2")
     og.recv(2)
     og.step(3)
+    ow_to_sibling(2)
+    ow_to_sibling(6)
     mark("w31")
     wg.third(1)
     mark("at2")
     ag.recv(2)
     ag.step(3)
+    turn_att(2)
+    turn_att(6)
+    for r in (1, 7, 2, 6):
+        ow_from_sibling(r)
+    near_product(0)
     mark("w32")
     wg.third(2)
+    near_product(1)
     mark("ow3")
     og.recv(3)
     og.step(4)
-    for r in (1, 7, 2, 6, 3, 5):
-        ow_to_sibling(r)
+    ow_to_sibling(3)
+    ow_to_sibling(5)
+    near_product(2)
     mark("w33")
     wg.third(3)
     mark("w40")
@@ -363,37 +390,30 @@
     mark("at3")
     ag.recv(3)
     ag.step(4)
+    near_product(3)
+    turn_att(3)
+    turn_att(5)
     mark("w41")
     wg.fourth(1)
+    near_product(4)
     mark("ow4")
     og.recv(4)
     ow_to_sibling(4)
-    mark("transpose")
-    for r in range(7):
-        att_t[:, r * HCOLS : (r + 1) * HCOLS] = attf[r * HCOLS : (r + 1) * HCOLS, :].T
-    mark("ow_sib")
-    for r in (1, 7, 2, 6, 3, 5):
-        ow_from_sibling(r)
-    mark("out_proj")
-
-    @pl.loop(0, 5)
-    def _(n):
-        cols_n = pl.ds(pl.multiple_of(n * 256, 256), 256)
-        hacc[:, cols_n] = pat[:, cols_n].astype(F32) + dot(att_t[...], owf[0 : 7 * HCOLS, cols_n])
-
     mark("w42")
     wg.fourth(2)
     wg.fourth(3)
+    for r in (3, 5):
+        ow_from_sibling(r)
     mark("at4")
     ag.recv(4)
     ow_from_sibling(4)
     mark("hidden")
-    att_u[...] = attf[7 * HCOLS : 8 * HCOLS, :].T
+    turn_att(4)
 
     @pl.loop(0, 5)
     def _(n):
         cols_n = pl.ds(pl.multiple_of(n * 256, 256), 256)
-        hid[:, cols_n] = (hacc[:, cols_n] + dot(att_u[...], owf[7 * HCOLS : 8 * HCOLS, cols_n])).astype(BF16)
+        hid[:, cols_n] = (hacc[:, cols_n] + dot(att_u[...], owf[5 * HCOLS : 8 * HCOLS, cols_n])).astype(BF16)
 
     mark("perm")
     spread_at = jnp.where(iota((SLOTS, 512), 0) == iota((SLOTS, 512), 1) // 4, 1.0, 0.0).astype(BF16)
@@ -424,11 +444,25 @@
         rows_send[2 * t] = eight[0:4, :].astype(BF16)
         rows_send[2 * t + 1] = eight[4:8, :].astype(BF16)
 
-    @pl.loop(1, N_CTX)
-    def _(d):
-        remote(
-            rows_send.at[other(d)], rows_in.at[ctx], rw_ss.at[d], rw_rs.at[d], {"ctx": other(d), "tp": z}
-        ).start()
+    def at_offset(dx, dy, dc):
+        x = (ctx // (2 * NY) + dx) % NX
+        y = ((ctx // 2) % NY + dy) % NY
+        return (x * NY + y) * 2 + (core + dc) % 2
+
+    hops = (0, 1, 2, 1)
+    offsets = sorted(
+        ((dx, dy, dc) for dx in range(4) for dy in range(4) for dc in range(2) if dx + dy + dc > 0),
+        key=lambda o: (-hops[o[0]] - hops[o[1]], o),
+    )
+
+    def row_copy(n, arriving):
+        dx, dy, dc = offsets[n]
+        to = at_offset(dx, dy, dc)
+        slot = at_offset(-dx % 4, -dy % 4, dc) if arriving else ctx
+        return remote(rows_send.at[to], rows_in.at[slot], rw_ss.at[n], rw_rs.at[n], {"ctx": to, "tp": z})
+
+    for n in range(len(offsets)):
+        row_copy(n, False).start()
 
     rows_in[ctx] = rows_send[ctx]
 
@@ -438,23 +472,31 @@
         return (x * NY + (x + zz) % NY) * 2 + zz // NY
 
     x_here = ctx // (2 * NY)
-    turn = ctx == source(z, x_here)
+    plane = (z - ((ctx // 2) % NY - x_here + NY) % NY - NY * core + NZ) % NZ
+    turn = (plane == 0) | (plane == 2)
+    half = plane // 2
+
+    def half_block(c, slot):
+        return (
+            colsend.at[pl.ds(pl.multiple_of(c * ROWS_W + (half % 2) * 80, 16), 80), :],
+            colin.at[pl.ds(pl.multiple_of(slot * 80, 16), 80), :],
+        )
+
+    def col_copy(n):
+        to = at_offset(*offsets[n])
+        slot = (half % 2) * 4 + x_here
+        src, dst = half_block(to, slot)
+        return remote(src, dst, co_ss.at[n], co_rs.at[slot], {"ctx": to, "tp": z})
 
     @pl.when(turn)
     def _():
         for n in range(40):
             colsend[n * 128 : (n + 1) * 128, :] = perm[:, n * 128 : (n + 1) * 128].T
 
-        @pl.loop(1, N_CTX)
-        def _(d):
-            remote(
-                block160(colsend, other(d)), block160(colin, x_here), co_ss.at[d], co_rs.at[x_here],
-                {"ctx": other(d), "tp": z},
-            ).start()
-
-        colin[pl.ds(pl.multiple_of(x_here * ROWS_W, 32), ROWS_W), :] = colsend[
-            pl.ds(pl.multiple_of(ctx * ROWS_W, 32), ROWS_W), :
-        ]
+        for n in range(len(offsets)):
+            col_copy(n).start()
+        mine = pl.ds(pl.multiple_of(ctx * ROWS_W + (half % 2) * 80, 16), 80)
+        colin[pl.ds(pl.multiple_of(((half % 2) * 4 + x_here) * 80, 16), 80), :] = colsend[mine, :]
 
     mark("idx_wait")
     @pl.loop(1, N_CTX)
@@ -506,11 +548,8 @@
 
     mark("rows_wait")
 
-    @pl.loop(1, N_CTX)
-    def _(d):
-        remote(
-            rows_send.at[other(d)], rows_in.at[behind(d)], rw_ss.at[d], rw_rs.at[d], {"ctx": other(d), "tp": z}
-        ).wait()
+    for n in range(len(offsets)):
+        row_copy(n, True).wait()
 
     mark("embed")
 
@@ -555,6 +594,31 @@
             cols_n = slice(128 * n, 128 * (n + 1))
             text[rows_b, cols_n] = jnp.where(taken, vision[:, cols_n].astype(BF16), text[rows_b, cols_n])
 
+    def col_region(r, part):
+        if part is None:
+            return colin.at[pl.ds(r * 640, 640), :]
+        return colin.at[pl.ds(r * 640 + part * 320, 320), :]
+
+    cg = Ring(p, col_region, cg_ss, cg_rs)
+
+    def turn_cols(r):
+        @pl.loop(0, 4)
+        def _(x):
+            for h, ref in ((0, colf), (1, colg)):
+                rows_s = pl.ds(pl.multiple_of(source((z + 2 * NZ - r - 2 * h) % NZ, x) * PITCH, 8), SLOTS)
+                came = colin[pl.ds(pl.multiple_of(r * 640 + (h * 4 + x) * 80, 16), 80), :].astype(F32)
+                ref[rows_s, :] = jnp.concatenate([came, jnp.zeros((48, 128), F32)], axis=0).T
+
+    mark("col_wait")
+    for h in range(2):
+        for x in range(4):
+
+            @pl.when(ctx != source((z + NZ - 2 * h) % NZ, x))
+            def _():
+                src, dst = half_block(0, h * 4 + x)
+                remote(src, dst, co_ss.at[0], co_rs.at[h * 4 + x], {"ctx": p.sib, "tp": z}).wait_recv()
+
+    cg.step(1)
     mark("stat_wait")
 
     @pl.loop(1, NZ)
@@ -602,9 +666,9 @@
     def order_block(t):
         for k in range(4):
             rows_k = pl.ds(pl.multiple_of(t * SLOTS + k * N_CTX, 32), N_CTX)
-            every = pl.ds(t * 4 + k, N_CTX, stride=SLOTS)
-            cols[rows_k, 0:128] = colf[every, :].astype(BF16)
-            cols[rows_k, 128:160] = colg[every, :][:, 0:32].astype(BF16)
+            every = pl.ds(t * 4 + k, N_CTX, stride=PITCH)
+            cols[rows_k, 0:80] = colf[every, :][:, 0:80].astype(BF16)
+            cols[rows_k, 80:160] = colg[every, :][:, 0:80].astype(BF16)
 
     def add_pair(i, j, first=False):
         base = gg.pair_rows(i, j)
@@ -614,55 +678,37 @@
         )
         grad_out[...] = part if first else grad_out[...] + part
 
-    def col_region(r, part):
-        if part is None:
-            return colin.at[pl.ds(r * 640, 640), :]
-        return colin.at[pl.ds(r * 640 + part * 320, 320), :]
-
-    cg = Ring(p, col_region, cg_ss, cg_rs)
-
-    def turn_cols(r):
-        @pl.loop(0, 4)
-        def _(x):
-            rows_s = pl.ds(pl.multiple_of(source((z + NZ - r) % NZ, x) * SLOTS, 128), SLOTS)
-            came = colin[pl.ds(pl.multiple_of((r * 4 + x) * ROWS_W, 32), ROWS_W), :].astype(F32)
-            colf[rows_s, :] = came[0:128, :].T
-            colg[rows_s, :] = jnp.concatenate([came[128:160, :], jnp.zeros((96, 128), F32)], axis=0).T
-
-    mark("col_wait")
-    for j in range(4):
-
-        @pl.when(ctx != source(z, j))
-        def _():
-            remote(
-                block160(colsend, ctx), block160(colin, j), co_ss.at[0], co_rs.at[j], {"ctx": p.sib, "tp": z}
-            ).wait_recv()
-
-    cg.step(1)
+    def pair(i, j, first=False):
+        base = gg.pair_rows(i, j) // SLOTS
+        for h in range(2):
+            order_block(base + h)
+        gg.from_sibling(i, j)
+        add_pair(i, j, first)
+
     mark("normed")
     normed_block(0)
     normed_block(1)
     normed_block(2)
     normed_block(3)
     turn_cols(0)
-    mark("g1")
-    gg.first()
     mark("c1")
     cg.recv(1)
     cg.step(2)
     mark("col_t")
     turn_cols(1)
     turn_cols(7)
-    mark("g2")
-    gg.second()
+    mark("g1")
+    gg.first()
+    mark("g30")
+    gg.third(0)
     mark("c2")
     cg.recv(2)
     cg.step(3)
-    mark("g30")
-    gg.third(0)
     mark("col_t")
     turn_cols(2)
     turn_cols(6)
+    mark("g2")
+    gg.second()
     mark("g31")
     gg.third(1)
     mark("c3")
@@ -677,42 +723,38 @@
     cg.recv(4)
     mark("col_t")
     turn_cols(4)
-    mark("order")
-
-    @pl.loop(0, N_CTX)
-    def _(t):
-        order_block(t)
-
-    mark("add1")
-    gg.from_sibling(0, 0)
-    add_pair(0, 0, True)
-    for i, j in ((1, 0), (0, 1)):
-        gg.from_sibling(i, j)
-        add_pair(i, j)
-    for i, j in ((2, 0), (0, 2)):
-        gg.from_sibling(i, j)
-        add_pair(i, j)
+    mark("add0")
+    pair(0, 0, True)
+    pair(1, 0)
+    pair(0, 1)
     mark("g33")
     gg.third(3)
-    for i, j in ((1, 1), (1, 2), (2, 1), (2, 2)):
-        gg.from_sibling(i, j)
-        add_pair(i, j)
+    mark("add1")
+    pair(2, 0)
+    pair(0, 2)
+    pair(1, 1)
     mark("g40")
     gg.fourth(0)
+    mark("add2")
+    pair(1, 2)
+    pair(2, 1)
+    pair(2, 2)
+    mark("g41")
     gg.fourth(1)
-    for i, j in ((3, 0), (0, 3), (3, 1), (1, 3)):
-        gg.from_sibling(i, j)
-        add_pair(i, j)
+    mark("add3")
+    pair(3, 0)
+    pair(0, 3)
     mark("g42")
     gg.fourth(2)
-    for i, j in ((3, 2), (2, 3)):
-        gg.from_sibling(i, j)
-        add_pair(i, j)
+    mark("add4")
+    pair(3, 1)
+    pair(1, 3)
     mark("g43")
     gg.fourth(3)
-    gg.from_sibling(3, 3)
-    add_pair(3, 3)
-
+    mark("add5")
+    pair(3, 2)
+    pair(2, 3)
+    pair(3, 3)
     mark("end")
     for b in range(4):
         normed_copy(b).wait()
@@ -723,19 +765,16 @@
 
     @pl.when(turn)
     def _():
-        @pl.loop(1, N_CTX)
-        def _(d):
-            remote(
-                block160(colsend, other(d)), block160(colin, x_here), co_ss.at[d], co_rs.at[0], {"ctx": other(d), "tp": z}
-            ).wait_send()
+        for n in range(len(offsets)):
+            col_copy(n).wait_send()
 
     mark(None)
 
 
 def hand_out(normed_in, grad_in, normed_out, grad_out, normed, grad, sem_in, sem_out):
     parts = [
-        (normed_in.at[pl.ds(r, 256), :], normed.at[pl.ds(r, 256), :], normed_out.at[pl.ds(r, 256), :])
-        for r in range(0, TOK, 256)
+        (normed_in.at[pl.ds(r, 128), :], normed.at[pl.ds(r, 128), :], normed_out.at[pl.ds(r, 128), :])
+        for r in range(0, TOK, 128)
     ] + [(grad_in, grad, grad_out)]
     come = [pltpu.make_async_copy(a, b, sem_in.at[n]) for n, (a, b, _) in enumerate(parts)]
     go = [pltpu.make_async_copy(b, c, sem_out.at[n]) for n, (_, b, c) in enumerate(parts)]
@@ -777,15 +816,15 @@
             pltpu.VMEM((N_CTX * SLOTS, 1024), BF16),
             pltpu.VMEM((DV, DV), BF16),
             pltpu.VMEM((DV, 512), BF16),
-            pltpu.VMEM((512, 7 * HCOLS), BF16),
-            pltpu.VMEM((512, HCOLS), BF16),
+            pltpu.VMEM((512, 5 * HCOLS), BF16),
+            pltpu.VMEM((512, 3 * HCOLS), BF16),
             pltpu.VMEM((512, DV), F32),
             pltpu.VMEM((512, DV), BF16),
             pltpu.VMEM((SLOTS, 4 * DV), BF16),
             pltpu.VMEM((4 * DV, SLOTS), BF16),
             pltpu.VMEM((N_CTX * ROWS_W, SLOTS), BF16),
-            pltpu.VMEM((N_CTX * SLOTS, 128), F32),
-            pltpu.VMEM((N_CTX * SLOTS, 128), F32),
+            pltpu.VMEM((N_CTX * PITCH, 128), F32),
+            pltpu.VMEM((N_CTX * PITCH, 128), F32),
             pltpu.VMEM((N_CTX * SLOTS, ROWS_W), BF16),
             pltpu.VMEM((TOK, 1024), BF16),
             pltpu.VMEM((TOK, 1024), BF16),
@@ -808,7 +847,7 @@
             dma((10,)),
             dma((36,)), dma((36,)), dma((36,)), dma((36,)),
             dma((8,)), dma((8,)), dma((8,)), dma((8,)), dma((8,)), dma((8,)),
-            dma((N_CTX,)), dma((N_CTX,)), dma((N_CTX,)), dma((N_CTX,)), dma((N_CTX,)), dma((4,)), dma((8,)), dma((8,)),
+            dma((N_CTX,)), dma((N_CTX,)), dma((N_CTX,)), dma((N_CTX,)), dma((N_CTX,)), dma((8,)), dma((8,)), dma((8,)),
             dma((NZ,)), dma((NZ,)),
         ],
         compiler_params=pltpu.CompilerParams(
@@ -836,8 +875,8 @@
         scratch_shapes=[
             pltpu.VMEM((TOK, 1024), BF16),
             pltpu.VMEM((ROWS_W, 1024), F32),
-            dma((5,)),
-            dma((5,)),
+            dma((9,)),
+            dma((9,)),
         ],
     )(*outs)
 

time: 105 us -> 95.3 us (0.908)
  Pallas kernels: 104 us -> 94.4 us
    pallas_call x1, Pallas kernels: 101 us -> 91.7 us  [shards(): pl.pallas_call(kernel, out_shape=(jax.ShapeDtypeStruct((TOK, 1024), BF16)...]
where the time goes in v3:
time: 95.3 us; the launch traced here: 95.2 us
  Pallas kernels  94.4 us (99%)
    pallas_call x1, Pallas kernels, shards(): pl.pallas_call(kernel, out_shape=(jax.ShapeDtypeStruct((TOK, 1024), BF16)...  91.7 us
    pallas_call x1, Pallas kernels, shards(): pl.pallas_call(hand_out, out_shape=(jax.ShapeDtypeStruct((TOK, 1024), BF1...  2.72 us

profile of v3, /device:TPU:1, one launch (start us, length us, event | category | flops | bytes accessed | tf_op | source)
XLA Modules:
  0.0 95.2 jit_solution(4435640192919705614)
XLA Ops:
  0.6 91.7 %shard_map.104 = (bf16[1024,1024]{1,0:T(8,128)(2,1)}, f32[160,1024]{1,0:T(8,128)}) custom-call(bf16[512,1280]{1,0:T(8,128)(2,1)} %pat_in.1, s32[1,512]{1,0:T(1,128)} %bitcast.5, s32[1,128]{1,0:T(1,128)} %bitcast.7, bf16[1024,1024]{1,0:T(8,128)(2,1)} %text_in.1, bf16[1024,1024]{1,0:T(8,128)(2,1)} %cot_in.1, bf16[3,160,1280]{2,1,0:T(8,128)(2,1)} %bitcast.4, ...), custom_call_target="tpu_custom_call" | custom-call | tf_op jit(solution)/shard_map/pallas_call | solution.py:804
  92.3 2.7 %shard_map.105 = (bf16[1024,1024]{1,0:T(8,128)(2,1)}, f32[160,1024]{1,0:T(8,128)}) custom-call(bf16[1024,1024]{1,0:T(8,128)(2,1)} %get-tuple-element.4.normed_in, f32[160,1024]{1,0:T(8,128)} %get-tuple-element.5.grad_in), custom_call_target="tpu_custom_call" | custom-call | tf_op jit(solution)/shard_map/pallas_call | solution.py:867

commit v4 on v3

--- a/solution.py
+++ b/solution.py
@@ -63,17 +63,18 @@
 
 
 class PlaneGather:
-    def __init__(self, place, buf, rows, ss, rs):
+    def __init__(self, place, buf, rows, ss, rs, part):
         self.p, self.buf, self.rows, self.half = place, buf, rows, rows // 2
-        self.ss, self.rs = ss, rs
+        self.ss, self.rs = ss.at[part], rs.at[part]
+        self.lanes = pl.ds(part * 512, 512)
         self.started = []
 
     def block(self, df, dg, part=None):
         base = self.p.near(df, dg) * self.rows
         if part is None:
-            return self.buf.at[pl.ds(pl.multiple_of(base, 32), self.rows), :]
+            return self.buf.at[pl.ds(pl.multiple_of(base, 32), self.rows), self.lanes]
         base = base + part * self.half
-        return self.buf.at[pl.ds(pl.multiple_of(base, 16), self.half), :]
+        return self.buf.at[pl.ds(pl.multiple_of(base, 16), self.half), self.lanes]
 
     def send(self, n, region, dev):
         c = remote(region, region, self.ss.at[n], self.rs.at[n], dev)
@@ -132,7 +133,7 @@
     def from_sibling(self, i, j):
         o = self.p.offs
         base = self.p.near(o[i], o[j]) + 1 - 2 * self.p.core
-        region = self.buf.at[pl.ds(pl.multiple_of(base * self.rows, 32), self.rows), :]
+        region = self.buf.at[pl.ds(pl.multiple_of(base * self.rows, 32), self.rows), self.lanes]
         self.recv(20 + 4 * j + i, region)
 
     def pair_rows(self, i, j):
@@ -175,8 +176,8 @@
 
 def kernel(
     pat_in, wid, pos, text_in, cot_in, qkv_in, ow_in, w_in, gain,
-    normed_out, grad_out,
-    pat, qkv, wf, gf, owf, attf, att_t, att_u, hacc, hid, perm, colsend, colin, colf, colg, cols, text, cot, normed,
+    normed, grad_out,
+    pat, qkv, wf, gf, owf, attf, att_t, att_u, att_v, hacc, hid, perm, colsend, colin, colf, colg, cols, text, cot,
     q0s, q1s, ks, vts, widc, mrow, rows_send, rows_in, incf, idx_send, idx_in, stats, cotsel, scol, drow,
     local, w_ss, w_rs, g_ss, g_rs, ow_ss, ow_rs, osib_ss, osib_rs, at_ss, at_rs,
     ix_ss, ix_rs, rw_ss, rw_rs, co_ss, co_rs, cg_ss, cg_rs, st_ss, st_rs,
@@ -267,9 +268,10 @@
     mark("barrier")
     pl.semaphore_wait(barrier, N_CTX - 1 + NZ - 1)
 
-    wg = PlaneGather(p, wf, ROWS_W, w_ss, w_rs)
+    w0, w1 = (PlaneGather(p, wf, ROWS_W, w_ss, w_rs, n) for n in range(2))
     load_w.wait()
-    wg.start()
+    w0.start()
+    w1.start()
 
     def place_of(r):
         return (0, 1, 7, 2, 6, 3, 5, 4).index(r)
@@ -328,23 +330,31 @@
         part = attf[k * HCOLS : (k + 1) * HCOLS, :].T
         if k < 5:
             att_t[:, k * HCOLS : (k + 1) * HCOLS] = part
+        elif k < 7:
+            att_u[:, (k - 5) * HCOLS : (k - 4) * HCOLS] = part
         else:
-            att_u[:, (k - 5) * HCOLS : (k - 4) * HCOLS] = part
+            att_v[...] = part
 
     def near_product(n):
         cols_n = slice(n * 256, (n + 1) * 256)
         hacc[:, cols_n] = pat[:, cols_n].astype(F32) + dot(att_t[...], owf[0 : 5 * HCOLS, cols_n])
 
+    def middle_product(n):
+        cols_n = slice(n * 256, (n + 1) * 256)
+        hacc[:, cols_n] += dot(att_u[:, 0 : 2 * HCOLS], owf[5 * HCOLS : 7 * HCOLS, cols_n])
+
     turn_att(0)
+    mark("w_first0")
+    w0.first()
+    w0.third(0)
     mark("ow1")
     og.recv(1)
     og.step(2)
     ow_to_sibling(1)
     ow_to_sibling(7)
-    mark("w_first")
-    wg.first()
-    mark("w30")
-    wg.third(0)
+    mark("w_first1")
+    w1.first()
+    w1.third(0)
     mark("at1")
     ag.recv(1)
     ag.step(2)
@@ -357,15 +367,21 @@
             idx_send.at[other(d)], idx_in.at[ctx], ix_ss.at[d], ix_rs.at[d], {"ctx": other(d), "tp": z}
         ).start()
 
-    mark("w_second")
-    wg.second()
+    mark("w_second0")
+    w0.second()
+    mark("w31_0")
+    w0.third(1)
+    mark("w_second1")
+    w1.second()
     mark("ow2")
     og.recv(2)
     og.step(3)
     ow_to_sibling(2)
     ow_to_sibling(6)
-    mark("w31")
-    wg.third(1)
+    mark("w32_0")
+    w0.third(2)
+    mark("w31_1")
+    w1.third(1)
     mark("at2")
     ag.recv(2)
     ag.step(3)
@@ -374,46 +390,58 @@
     for r in (1, 7, 2, 6):
         ow_from_sibling(r)
     near_product(0)
-    mark("w32")
-    wg.third(2)
+    mark("w32_1")
+    w1.third(2)
     near_product(1)
+    mark("w33_0")
+    w0.third(3)
     mark("ow3")
     og.recv(3)
     og.step(4)
     ow_to_sibling(3)
     ow_to_sibling(5)
     near_product(2)
-    mark("w33")
-    wg.third(3)
-    mark("w40")
-    wg.fourth(0)
+    mark("w33_1")
+    w1.third(3)
+    mark("w40_0")
+    w0.fourth(0)
+    w0.fourth(1)
+    near_product(3)
     mark("at3")
     ag.recv(3)
     ag.step(4)
-    near_product(3)
     turn_att(3)
     turn_att(5)
-    mark("w41")
-    wg.fourth(1)
+    mark("w40_1")
+    w1.fourth(0)
+    w1.fourth(1)
     near_product(4)
+    for r in (3, 5):
+        ow_from_sibling(r)
+    middle_product(0)
+    middle_product(1)
     mark("ow4")
     og.recv(4)
     ow_to_sibling(4)
-    mark("w42")
-    wg.fourth(2)
-    wg.fourth(3)
-    for r in (3, 5):
-        ow_from_sibling(r)
+    middle_product(2)
+    mark("w42_0")
+    w0.fourth(2)
+    w0.fourth(3)
+    middle_product(3)
+    middle_product(4)
     mark("at4")
     ag.recv(4)
     ow_from_sibling(4)
+    mark("w42_1")
+    w1.fourth(2)
+    w1.fourth(3)
     mark("hidden")
     turn_att(4)
 
     @pl.loop(0, 5)
     def _(n):
         cols_n = pl.ds(pl.multiple_of(n * 256, 256), 256)
-        hid[:, cols_n] = (hacc[:, cols_n] + dot(att_u[...], owf[5 * HCOLS : 8 * HCOLS, cols_n])).astype(BF16)
+        hid[:, cols_n] = (hacc[:, cols_n] + dot(att_v[...], owf[7 * HCOLS : 8 * HCOLS, cols_n])).astype(BF16)
 
     mark("perm")
     spread_at = jnp.where(iota((SLOTS, 512), 0) == iota((SLOTS, 512), 1) // 4, 1.0, 0.0).astype(BF16)
@@ -426,24 +454,6 @@
                 select, hid[:, n * 256 : (n + 1) * 256]
             ).astype(BF16)
 
-    mark("w_sib")
-    for i in range(4):
-        for j in range(4):
-            wg.from_sibling(i, j)
-
-    mark("merge")
-    @pl.loop(0, 4)
-    def _(n):
-        cols_n = pl.ds(pl.multiple_of(n * 256, 256), 256)
-        mrow[:, cols_n] = dot(perm[...], wf[:, cols_n]).astype(BF16).astype(F32)
-
-    mark("rows_send")
-    @pl.loop(0, N_CTX // 2)
-    def _(t):
-        eight = mrow[pl.ds(pl.multiple_of(t * 8, 8), 8), :]
-        rows_send[2 * t] = eight[0:4, :].astype(BF16)
-        rows_send[2 * t + 1] = eight[4:8, :].astype(BF16)
-
     def at_offset(dx, dy, dc):
         x = (ctx // (2 * NY) + dx) % NX
         y = ((ctx // 2) % NY + dy) % NY
@@ -455,14 +465,35 @@
         key=lambda o: (-hops[o[0]] - hops[o[1]], o),
     )
 
-    def row_copy(n, arriving):
+    def row_copy(n, part, arriving):
         dx, dy, dc = offsets[n]
         to = at_offset(dx, dy, dc)
         slot = at_offset(-dx % 4, -dy % 4, dc) if arriving else ctx
-        return remote(rows_send.at[to], rows_in.at[slot], rw_ss.at[n], rw_rs.at[n], {"ctx": to, "tp": z})
-
-    for n in range(len(offsets)):
-        row_copy(n, False).start()
+        lanes = pl.ds(part * 512, 512)
+        return remote(
+            rows_send.at[to, :, lanes], rows_in.at[slot, :, lanes], rw_ss.at[part, n], rw_rs.at[part, n],
+            {"ctx": to, "tp": z},
+        )
+
+    for part, w in ((0, w0), (1, w1)):
+        mark("w_sib")
+        for i in range(4):
+            for j in range(4):
+                w.from_sibling(i, j)
+        mark("merge")
+        for n in (2 * part, 2 * part + 1):
+            cols_n = slice(256 * n, 256 * (n + 1))
+            mrow[:, cols_n] = dot(perm[...], wf[:, cols_n]).astype(BF16).astype(F32)
+        lanes = slice(512 * part, 512 * (part + 1))
+
+        @pl.loop(0, N_CTX // 2, unroll=4)
+        def _(t):
+            eight = mrow[pl.ds(pl.multiple_of(t * 8, 8), 8), lanes]
+            rows_send[2 * t, :, lanes] = eight[0:4, :].astype(BF16)
+            rows_send[2 * t + 1, :, lanes] = eight[4:8, :].astype(BF16)
+
+        for n in range(len(offsets)):
+            row_copy(n, part, False).start()
 
     rows_in[ctx] = rows_send[ctx]
 
@@ -548,8 +579,9 @@
 
     mark("rows_wait")
 
-    for n in range(len(offsets)):
-        row_copy(n, True).wait()
+    for part in range(2):
+        for n in range(len(offsets)):
+            row_copy(n, part, True).wait()
 
     mark("embed")
 
@@ -646,12 +678,9 @@
         gained = gain_of(n) * cotsel[:, cols_n]
         gf[own_g, cols_n] = (s_at * gained - incf[:, cols_n] * (s_at * s_at * s_at) * i_at / D).astype(BF16)
 
-    gg = PlaneGather(p, gf, SLOTS, g_ss, g_rs)
-    gg.start()
-
-    def normed_copy(b):
-        rows_b = pl.ds(pl.multiple_of(b * 256, 256), 256)
-        return pltpu.make_async_copy(normed.at[rows_b, :], normed_out.at[rows_b, :], local.at[4 + b])
+    g0, g1 = (PlaneGather(p, gf, SLOTS, g_ss, g_rs, n) for n in range(2))
+    g0.start()
+    g1.start()
 
     def normed_block(b):
         for h in range(2):
@@ -661,7 +690,6 @@
                 normed[rows_b, cols_n] = (
                     text[rows_b, cols_n].astype(F32) * scol[rows_b, :] * gain_of(n)
                 ).astype(BF16)
-        normed_copy(b).start()
 
     def order_block(t):
         for k in range(4):
@@ -671,7 +699,7 @@
             cols[rows_k, 80:160] = colg[every, :][:, 0:80].astype(BF16)
 
     def add_pair(i, j, first=False):
-        base = gg.pair_rows(i, j)
+        base = g0.pair_rows(i, j)
         rows_p = pl.ds(pl.multiple_of(base, 256), 256)
         part = lax.dot_general(
             cols[rows_p, :], gf[rows_p, :], (((0,), (0,)), ((), ())), preferred_element_type=F32
@@ -679,10 +707,11 @@
         grad_out[...] = part if first else grad_out[...] + part
 
     def pair(i, j, first=False):
-        base = gg.pair_rows(i, j) // SLOTS
+        base = g0.pair_rows(i, j) // SLOTS
         for h in range(2):
             order_block(base + h)
-        gg.from_sibling(i, j)
+        g0.from_sibling(i, j)
+        g1.from_sibling(i, j)
         add_pair(i, j, first)
 
     mark("normed")
@@ -694,71 +723,85 @@
     mark("c1")
     cg.recv(1)
     cg.step(2)
+    mark("g1_0")
+    g0.first()
+    g0.third(0)
     mark("col_t")
     turn_cols(1)
     turn_cols(7)
-    mark("g1")
-    gg.first()
-    mark("g30")
-    gg.third(0)
+    mark("g1_1")
+    g1.first()
+    g1.third(0)
     mark("c2")
     cg.recv(2)
     cg.step(3)
+    mark("g2_0")
+    g0.second()
+    mark("g31_0")
+    g0.third(1)
     mark("col_t")
     turn_cols(2)
     turn_cols(6)
-    mark("g2")
-    gg.second()
-    mark("g31")
-    gg.third(1)
+    mark("g2_1")
+    g1.second()
+    mark("g32_0")
+    g0.third(2)
+    mark("g31_1")
+    g1.third(1)
     mark("c3")
     cg.recv(3)
     cg.step(4)
     mark("col_t")
     turn_cols(3)
     turn_cols(5)
-    mark("g32")
-    gg.third(2)
+    mark("g32_1")
+    g1.third(2)
+    mark("g33_0")
+    g0.third(3)
     mark("c4")
     cg.recv(4)
+    mark("g33_1")
+    g1.third(3)
     mark("col_t")
     turn_cols(4)
     mark("add0")
     pair(0, 0, True)
     pair(1, 0)
     pair(0, 1)
-    mark("g33")
-    gg.third(3)
+    mark("g40_0")
+    g0.fourth(0)
+    g0.fourth(1)
     mark("add1")
     pair(2, 0)
     pair(0, 2)
     pair(1, 1)
-    mark("g40")
-    gg.fourth(0)
+    mark("g40_1")
+    g1.fourth(0)
+    g1.fourth(1)
     mark("add2")
     pair(1, 2)
     pair(2, 1)
     pair(2, 2)
-    mark("g41")
-    gg.fourth(1)
+    mark("g42_0")
+    g0.fourth(2)
     mark("add3")
     pair(3, 0)
     pair(0, 3)
-    mark("g42")
-    gg.fourth(2)
+    mark("g42_1")
+    g1.fourth(2)
+    mark("g43_0")
+    g0.fourth(3)
     mark("add4")
     pair(3, 1)
     pair(1, 3)
-    mark("g43")
-    gg.fourth(3)
+    mark("g43_1")
+    g1.fourth(3)
     mark("add5")
     pair(3, 2)
     pair(2, 3)
     pair(3, 3)
     mark("end")
-    for b in range(4):
-        normed_copy(b).wait()
-    for c in (wg, gg, og, ag, cg):
+    for c in (w0, w1, g0, g1, og, ag, cg):
         c.finish()
     for c in osib:
         c.wait_send()
@@ -771,17 +814,12 @@
     mark(None)
 
 
-def hand_out(normed_in, grad_in, normed_out, grad_out, normed, grad, sem_in, sem_out):
-    parts = [
-        (normed_in.at[pl.ds(r, 128), :], normed.at[pl.ds(r, 128), :], normed_out.at[pl.ds(r, 128), :])
-        for r in range(0, TOK, 128)
-    ] + [(grad_in, grad, grad_out)]
-    come = [pltpu.make_async_copy(a, b, sem_in.at[n]) for n, (a, b, _) in enumerate(parts)]
-    go = [pltpu.make_async_copy(b, c, sem_out.at[n]) for n, (_, b, c) in enumerate(parts)]
-    for c in come:
-        c.start()
-    for c, g in zip(come, go):
-        c.wait()
+def hand_out(normed, grad, normed_out, grad_out, sems):
+    go = [
+        pltpu.make_async_copy(normed, normed_out, sems.at[0]),
+        pltpu.make_async_copy(grad, grad_out, sems.at[1]),
+    ]
+    for g in go:
         g.start()
     for g in go:
         g.wait()
@@ -803,12 +841,9 @@
     dma = pltpu.SemaphoreType.DMA
     outs = pl.pallas_call(
         kernel,
-        out_shape=(
-            jax.ShapeDtypeStruct((TOK, 1024), BF16),
-            jax.ShapeDtypeStruct((ROWS_W, 1024), F32),
-        ),
+        out_shape=(pltpu.VMEM((TOK, 1024), BF16), pltpu.VMEM((ROWS_W, 1024), F32)),
         in_specs=[anywhere, vmem, vmem, anywhere, anywhere, anywhere, anywhere, anywhere, vmem],
-        out_specs=(anywhere, vmem),
+        out_specs=(vmem, vmem),
         scratch_shapes=[
             pltpu.VMEM((512, DV), BF16),
             pltpu.VMEM((3, HCOLS, DV), BF16),
@@ -817,7 +852,8 @@
             pltpu.VMEM((DV, DV), BF16),
             pltpu.VMEM((DV, 512), BF16),
             pltpu.VMEM((512, 5 * HCOLS), BF16),
-            pltpu.VMEM((512, 3 * HCOLS), BF16),
+            pltpu.VMEM((512, 2 * HCOLS), BF16),
+            pltpu.VMEM((512, HCOLS), BF16),
             pltpu.VMEM((512, DV), F32),
             pltpu.VMEM((512, DV), BF16),
             pltpu.VMEM((SLOTS, 4 * DV), BF16),
@@ -826,7 +862,6 @@
             pltpu.VMEM((N_CTX * PITCH, 128), F32),
             pltpu.VMEM((N_CTX * PITCH, 128), F32),
             pltpu.VMEM((N_CTX * SLOTS, ROWS_W), BF16),
-            pltpu.VMEM((TOK, 1024), BF16),
             pltpu.VMEM((TOK, 1024), BF16),
             pltpu.VMEM((TOK, 1024), BF16),
             pltpu.VMEM((512, HCOLS), BF16),
@@ -845,13 +880,13 @@
             pltpu.VMEM((TOK, SLOTS), F32),
             pltpu.VMEM((SLOTS, TOK), BF16),
             dma((10,)),
-            dma((36,)), dma((36,)), dma((36,)), dma((36,)),
+            dma((2, 36)), dma((2, 36)), dma((2, 36)), dma((2, 36)),
             dma((8,)), dma((8,)), dma((8,)), dma((8,)), dma((8,)), dma((8,)),
-            dma((N_CTX,)), dma((N_CTX,)), dma((N_CTX,)), dma((N_CTX,)), dma((N_CTX,)), dma((8,)), dma((8,)), dma((8,)),
+            dma((N_CTX,)), dma((N_CTX,)), dma((2, N_CTX)), dma((2, N_CTX)), dma((N_CTX,)), dma((8,)), dma((8,)), dma((8,)),
             dma((NZ,)), dma((NZ,)),
         ],
         compiler_params=pltpu.CompilerParams(
-            collective_id=0, has_side_effects=True, vmem_limit_bytes=62 * 1024 * 1024
+            collective_id=0, has_side_effects=True, vmem_limit_bytes=56 * 1024 * 1024
         ),
     )(
         patches,
@@ -873,11 +908,9 @@
         in_specs=[anywhere, anywhere],
         out_specs=(anywhere, anywhere),
         scratch_shapes=[
-            pltpu.VMEM((TOK, 1024), BF16),
-            pltpu.VMEM((ROWS_W, 1024), F32),
-            dma((9,)),
-            dma((9,)),
+            dma((2,)),
         ],
+        compiler_params=pltpu.CompilerParams(vmem_limit_bytes=1024 * 1024),
     )(*outs)
 
 

time: 95.3 us -> 91.5 us (0.960)
  Pallas kernels: 94.4 us -> 90.5 us
    pallas_call x1, Pallas kernels: 91.7 us -> 89 us  [shards(): pl.pallas_call(kernel, out_shape=(pltpu.VMEM((TOK, 1024), BF16), pltpu.VM...]
    pallas_call x1, Pallas kernels: 2.72 us -> 1.55 us  [shards(): pl.pallas_call(hand_out, out_shape=(jax.ShapeDtypeStruct((TOK, 1024), BF1...]
where the time goes in v4:
time: 91.5 us; the launch traced here: 91.3 us
  Pallas kernels  90.5 us (99%)
    pallas_call x1, Pallas kernels, shards(): pl.pallas_call(kernel, out_shape=(pltpu.VMEM((TOK, 1024), BF16), pltpu.VM...  89 us

profile of v4, /device:TPU:1, one launch (start us, length us, event | category | flops | bytes accessed | tf_op | source)
XLA Modules:
  0.0 91.3 jit_solution(14869797102210691534)
XLA Ops:
  0.6 89.0 %shard_map.104 = (bf16[1024,1024]{1,0:T(8,128)(2,1)S(1)}, f32[160,1024]{1,0:T(8,128)S(1)}) custom-call(bf16[512,1280]{1,0:T(8,128)(2,1)} %pat_in.1, s32[1,512]{1,0:T(1,128)} %bitcast.5, s32[1,128]{1,0:T(1,128)} %bitcast.7, bf16[1024,1024]{1,0:T(8,128)(2,1)} %text_in.1, bf16[1024,1024]{1,0:T(8,128)(2,1)} %cot_in.1, bf16[3,160,1280]{2,1,0:T(8,128)(2,1)} %bitcast.4, ...), custom_call_target="tpu_custom_call" | custom-call | tf_op jit(solution)/shard_map/pallas_call | solution.py:842
  89.6 1.5 %shard_map.105 = (bf16[1024,1024]{1,0:T(8,128)(2,1)}, f32[160,1024]{1,0:T(8,128)}) custom-call(bf16[1024,1024]{1,0:T(8,128)(2,1)S(1)} %get-tuple-element.4.normed, f32[160,1024]{1,0:T(8,128)S(1)} %get-tuple-element.5.grad), custom_call_target="tpu_custom_call" | custom-call | tf_op jit(solution)/shard_map/pallas_call | solution.py:902

commit v5 on v4

--- a/solution.py
+++ b/solution.py
@@ -175,9 +175,9 @@
 
 
 def kernel(
-    pat_in, wid, pos, text_in, cot_in, qkv_in, ow_in, w_in, gain,
+    pat_in, wid_in, pos_in, text_in, cot_in, qkv_in, ow_in, w_in, gain_in,
     normed, grad_out,
-    pat, qkv, wf, gf, owf, attf, att_t, att_u, att_v, hacc, hid, perm, colsend, colin, colf, colg, cols, text, cot,
+    wid, pos, gain, sel, pat, qkv, wf, gf, owf, attf, att_t, att_u, att_v, hacc, perm, colsend, colin, colf, colg, cols, text, cot,
     q0s, q1s, ks, vts, widc, mrow, rows_send, rows_in, incf, idx_send, idx_in, stats, cotsel, scol, drow,
     local, w_ss, w_rs, g_ss, g_rs, ow_ss, ow_rs, osib_ss, osib_rs, at_ss, at_rs,
     ix_ss, ix_rs, rw_ss, rw_rs, co_ss, co_rs, cg_ss, cg_rs, st_ss, st_rs,
@@ -201,24 +201,28 @@
             scope[-1].__enter__()
 
     mark("index")
+    def block160(ref, c):
+        return ref.at[pl.ds(pl.multiple_of(c * ROWS_W, 32), ROWS_W), :]
+
+    barrier = pltpu.get_barrier_semaphore()
+
+    @pl.loop(1, N_CTX)
+    def _(d):
+        pl.semaphore_signal(barrier, inc=1, device_id={"ctx": other(d), "tp": z}, device_id_type=MESH)
+
+    @pl.loop(1, NZ)
+    def _(d):
+        pl.semaphore_signal(barrier, inc=1, device_id={"ctx": ctx, "tp": (z + d) % NZ}, device_id_type=MESH)
+
+    load_pos = pltpu.make_async_copy(pos_in, pos, local.at[10])
+    load_wid = pltpu.make_async_copy(wid_in, wid, local.at[11])
+    load_gain = pltpu.make_async_copy(gain_in, gain, local.at[12])
+    load_pos.start()
+    load_wid.start()
     load_pat = pltpu.make_async_copy(pat_in, pat, local.at[8])
     load_qkv = pltpu.make_async_copy(qkv_in, qkv, local.at[9])
     load_pat.start()
     load_qkv.start()
-
-    def block160(ref, c):
-        return ref.at[pl.ds(pl.multiple_of(c * ROWS_W, 32), ROWS_W), :]
-
-    barrier = pltpu.get_barrier_semaphore()
-
-    @pl.loop(1, N_CTX)
-    def _(d):
-        pl.semaphore_signal(barrier, inc=1, device_id={"ctx": other(d), "tp": z}, device_id_type=MESH)
-
-    @pl.loop(1, NZ)
-    def _(d):
-        pl.semaphore_signal(barrier, inc=1, device_id={"ctx": ctx, "tp": (z + d) % NZ}, device_id_type=MESH)
-
     own_w = wf.at[pl.ds(pl.multiple_of(ctx * ROWS_W, 32), ROWS_W), :]
     own_ow = owf.at[pl.ds(0, HCOLS), :]
     load_w = pltpu.make_async_copy(w_in, own_w, local.at[0])
@@ -229,6 +233,9 @@
     load_ow.start()
     load_text.start()
     load_cot.start()
+    load_gain.start()
+    load_pos.wait()
+    load_wid.wait()
 
     pos_row = pos[...]
     pos_col = jnp.broadcast_to(pos_row, (SLOTS, SLOTS)).T
@@ -251,6 +258,12 @@
     for t in range(N_CTX):
         idx_send[t] = jnp.broadcast_to(index_rows[t : t + 1, :], (8, SLOTS))
     idx_in[ctx] = idx_send[ctx]
+
+    spread_at = jnp.where(iota((SLOTS, 512), 0) == iota((SLOTS, 512), 1) // 4, 1.0, 0.0).astype(BF16)
+    bucket512 = dot(jnp.broadcast_to(bucket_row, (8, SLOTS)).astype(BF16), spread_at)[0:1, :]
+    chosen = iota((SLOTS, 512), 0).astype(F32) == bucket512
+    for i in range(4):
+        sel[i] = jnp.where(chosen & (iota((SLOTS, 512), 1) % 4 == i), 1.0, 0.0).astype(BF16)
 
     for b in range(4):
         widc[128 * b : 128 * (b + 1), :] = jnp.broadcast_to(wid[:, 128 * b : 128 * (b + 1)], (128, 128)).T
@@ -438,21 +451,11 @@
     mark("hidden")
     turn_att(4)
 
-    @pl.loop(0, 5)
-    def _(n):
-        cols_n = pl.ds(pl.multiple_of(n * 256, 256), 256)
-        hid[:, cols_n] = (hacc[:, cols_n] + dot(att_v[...], owf[7 * HCOLS : 8 * HCOLS, cols_n])).astype(BF16)
-
-    mark("perm")
-    spread_at = jnp.where(iota((SLOTS, 512), 0) == iota((SLOTS, 512), 1) // 4, 1.0, 0.0).astype(BF16)
-    bucket512 = dot(jnp.broadcast_to(bucket_row, (8, SLOTS)).astype(BF16), spread_at)[0:1, :]
-    chosen = iota((SLOTS, 512), 0).astype(F32) == bucket512
-    for i in range(4):
-        select = jnp.where(chosen & (iota((SLOTS, 512), 1) % 4 == i), 1.0, 0.0).astype(BF16)
-        for n in range(5):
-            perm[:, i * DV + n * 256 : i * DV + (n + 1) * 256] = dot(
-                select, hid[:, n * 256 : (n + 1) * 256]
-            ).astype(BF16)
+    for n in range(5):
+        cols_n = slice(n * 256, (n + 1) * 256)
+        hidden = (hacc[:, cols_n] + dot(att_v[...], owf[7 * HCOLS : 8 * HCOLS, cols_n])).astype(BF16)
+        for i in range(4):
+            perm[:, i * DV + n * 256 : i * DV + (n + 1) * 256] = dot(sel[i], hidden).astype(BF16)
 
     def at_offset(dx, dy, dc):
         x = (ctx // (2 * NY) + dx) % NX
@@ -551,6 +554,7 @@
         cols_n = pl.ds(pl.multiple_of(n * 256, 256), 256)
         cotsel[:, cols_n] = dot(drow[...], cot[:, cols_n])
 
+    load_gain.wait()
     gains = gain[...].astype(F32)
 
     def gain_of(n):
@@ -816,9 +820,9 @@
 
 def hand_out(normed, grad, normed_out, grad_out, sems):
     go = [
-        pltpu.make_async_copy(normed, normed_out, sems.at[0]),
-        pltpu.make_async_copy(grad, grad_out, sems.at[1]),
-    ]
+        pltpu.make_async_copy(normed.at[pl.ds(r, 256), :], normed_out.at[pl.ds(r, 256), :], sems.at[r // 256])
+        for r in range(0, TOK, 256)
+    ] + [pltpu.make_async_copy(grad, grad_out, sems.at[4])]
     for g in go:
         g.start()
     for g in go:
@@ -842,9 +846,13 @@
     outs = pl.pallas_call(
         kernel,
         out_shape=(pltpu.VMEM((TOK, 1024), BF16), pltpu.VMEM((ROWS_W, 1024), F32)),
-        in_specs=[anywhere, vmem, vmem, anywhere, anywhere, anywhere, anywhere, anywhere, vmem],
+        in_specs=[anywhere] * 9,
         out_specs=(vmem, vmem),
         scratch_shapes=[
+            pltpu.VMEM((1, 512), jnp.int32),
+            pltpu.VMEM((1, SLOTS), jnp.int32),
+            pltpu.VMEM((8, 128), BF16),
+            pltpu.VMEM((4, SLOTS, 512), BF16),
             pltpu.VMEM((512, DV), BF16),
             pltpu.VMEM((3, HCOLS, DV), BF16),
             pltpu.VMEM((N_CTX * ROWS_W, 1024), BF16),
@@ -855,7 +863,6 @@
             pltpu.VMEM((512, 2 * HCOLS), BF16),
             pltpu.VMEM((512, HCOLS), BF16),
             pltpu.VMEM((512, DV), F32),
-            pltpu.VMEM((512, DV), BF16),
             pltpu.VMEM((SLOTS, 4 * DV), BF16),
             pltpu.VMEM((4 * DV, SLOTS), BF16),
             pltpu.VMEM((N_CTX * ROWS_W, SLOTS), BF16),
@@ -879,7 +886,7 @@
             pltpu.VMEM((SLOTS, 1024), F32),
             pltpu.VMEM((TOK, SLOTS), F32),
             pltpu.VMEM((SLOTS, TOK), BF16),
-            dma((10,)),
+            dma((13,)),
             dma((2, 36)), dma((2, 36)), dma((2, 36)), dma((2, 36)),
             dma((8,)), dma((8,)), dma((8,)), dma((8,)), dma((8,)), dma((8,)),
             dma((N_CTX,)), dma((N_CTX,)), dma((2, N_CTX)), dma((2, N_CTX)), dma((N_CTX,)), dma((8,)), dma((8,)), dma((8,)),
@@ -908,7 +915,7 @@
         in_specs=[anywhere, anywhere],
         out_specs=(anywhere, anywhere),
         scratch_shapes=[
-            dma((2,)),
+            dma((5,)),
         ],
         compiler_params=pltpu.CompilerParams(vmem_limit_bytes=1024 * 1024),
     )(*outs)

time: 91.5 us -> 91.6 us (level)
  no operation moved by 1% of the time
where the time goes in v5:
time: 91.6 us; the launch traced here: 91.5 us
  Pallas kernels  90.7 us (99%)
    pallas_call x1, Pallas kernels, shards(): pl.pallas_call(kernel, out_shape=(pltpu.VMEM((TOK, 1024), BF16), pltpu.VM...  89.1 us

profile of v5, /device:TPU:1, one launch (start us, length us, event | category | flops | bytes accessed | tf_op | source)
XLA Modules:
  0.0 91.5 jit_solution(15378396418572569398)
XLA Ops:
  0.6 89.1 %shard_map.104 = (bf16[1024,1024]{1,0:T(8,128)(2,1)S(1)}, f32[160,1024]{1,0:T(8,128)S(1)}) custom-call(bf16[512,1280]{1,0:T(8,128)(2,1)} %pat_in.1, s32[1,512]{1,0:T(1,128)} %bitcast.5, s32[1,128]{1,0:T(1,128)} %bitcast.7, bf16[1024,1024]{1,0:T(8,128)(2,1)} %text_in.1, bf16[1024,1024]{1,0:T(8,128)(2,1)} %cot_in.1, bf16[3,160,1280]{2,1,0:T(8,128)(2,1)} %bitcast.4, ...), custom_call_target="tpu_custom_call" | custom-call | tf_op jit(solution)/shard_map/pallas_call | solution.py:846
  89.7 1.6 %shard_map.105 = (bf16[1024,1024]{1,0:T(8,128)(2,1)}, f32[160,1024]{1,0:T(8,128)}) custom-call(bf16[1024,1024]{1,0:T(8,128)(2,1)S(1)} %get-tuple-element.4.normed, f32[160,1024]{1,0:T(8,128)S(1)} %get-tuple-element.5.grad), custom_call_target="tpu_custom_call" | custom-call | tf_op jit(solution)/shard_map/pallas_call | solution.py:909
